TPU v7x, 32 devices: a 4x4x1 block of a 4x4x8 slice. The times are simulated.
32 devices in a mesh: data: 1 (over z), col: 4 (over y), row: 8 (over x, core).
Axes of the slice: x: 4, y: 4, z: 1, core: 2. Of those that a mesh axis runs over, the one named last changes fastest.
The devices are a block of a 4x4x8 slice.
Arguments:
- x_seq: bfloat16 [24, 32, 4096], P(None, 'data', 'row')
- h_init: float32 [2, 32, 4096], P(None, 'data', 'row')
- wx_l1: bfloat16 [4096, 3, 4096], P('row', None, 'col')
- whru_l1: bfloat16 [4096, 2, 4096], P('row', None, 'col')
- whn_l1: bfloat16 [4096, 4096], P('row', 'col')
- bias_l1: float32 [3, 4096], P(None, 'col')
- wx_l2: bfloat16 [4096, 3, 4096], P('row', None, 'col')
- whru_l2: bfloat16 [4096, 2, 4096], P('row', None, 'col')
- whn_l2: bfloat16 [4096, 4096], P('row', 'col')
- bias_l2: float32 [3, 4096], P(None, 'col')
Outputs:
- output 1: bfloat16 [24, 32, 4096], P(None, 'data', ('col', 'row'))
- output 2: float32 [2, 32, 4096], P(None, 'data', ('col', 'row'))
All inputs are finite; a program needn't handle non-finite values.
Results may differ from a plain program's by a relative error of at most 0.0024724.
Values are sent between devices in bfloat16 or wider.
A program may use at most 768 MiB of HBM per device.

v0:
```python
import jax
import jax.numpy as jnp
from jax import lax
from jax.sharding import PartitionSpec as P


def solution(mesh):
    row_count = mesh.shape["row"]
    seq_spec = P(None, "data", "row")
    out_spec = P(None, "data", ("col", "row"))
    wide_spec = P("row", None, "col")
    square_spec = P("row", "col")
    bias_spec = P(None, "col")

    def gather_rows(col_part, row_idx, row_block):
        gathered = lax.all_gather(col_part, "col", axis=1, tiled=True)
        return lax.dynamic_slice_in_dim(gathered, row_idx * row_block, row_block, axis=1)

    def own_part(col_part, row_idx):
        unit_block = col_part.shape[-1] // row_count
        return lax.dynamic_slice_in_dim(col_part, row_idx * unit_block, unit_block, axis=col_part.ndim - 1)

    def gru_layer(in_rows, h_col, h_row, w_x, w_hru, w_hn, gate_bias, keep_rows):
        row_idx = lax.axis_index("row")
        row_block = in_rows.shape[2]

        def gru_step(state_pair, step_in):
            h_prev, prev_row = state_pair
            in_part = jnp.einsum("bk,kgn->bgn", step_in, w_x, preferred_element_type=jnp.float32)
            rec_part = jnp.einsum("bk,kgn->bgn", prev_row, w_hru, preferred_element_type=jnp.float32)
            part_sum = jnp.concatenate([in_part[:, :2] + rec_part, in_part[:, 2:]], axis=1)
            gate_pre = lax.psum(part_sum, "row") + gate_bias
            reset_gate = jax.nn.sigmoid(gate_pre[:, 0])
            update_gate = jax.nn.sigmoid(gate_pre[:, 1])
            gated_row = gather_rows((reset_gate * h_prev).astype(jnp.bfloat16), row_idx, row_block)
            cand_pre = lax.psum(jnp.dot(gated_row, w_hn, preferred_element_type=jnp.float32), "row")
            candidate = jnp.tanh(gate_pre[:, 2] + cand_pre)
            h_next = (1.0 - update_gate) * candidate + update_gate * h_prev
            next_row = gather_rows(h_next.astype(jnp.bfloat16), row_idx, row_block)
            if keep_rows:
                step_out = next_row
            else:
                step_out = own_part(h_next, row_idx).astype(jnp.bfloat16)
            return (h_next, next_row), step_out

        final_pair, seq_out = lax.scan(gru_step, (h_col, h_row), in_rows)
        return final_pair[0], seq_out

    def device_body(x_rows, h_rows, wx_l1, whru_l1, whn_l1, bias_l1, wx_l2, whru_l2, whn_l2, bias_l2):
        row_idx = lax.axis_index("row")
        col_idx = lax.axis_index("col")
        col_block = wx_l1.shape[2]
        h_gathered = lax.all_gather(h_rows, "row", axis=2, tiled=True)
        h_cols = lax.dynamic_slice_in_dim(h_gathered, col_idx * col_block, col_block, axis=2)
        h_starts = h_rows.astype(jnp.bfloat16)
        h1_last, h1_rows = gru_layer(x_rows, h_cols[0], h_starts[0], wx_l1, whru_l1, whn_l1, bias_l1, True)
        h2_last, h2_own = gru_layer(h1_rows, h_cols[1], h_starts[1], wx_l2, whru_l2, whn_l2, bias_l2, False)
        h_final = jnp.stack([own_part(h1_last, row_idx), own_part(h2_last, row_idx)])
        return h2_own, h_final

    return jax.shard_map(
        device_body,
        mesh=mesh,
        in_specs=(seq_spec, seq_spec, wide_spec, wide_spec, square_spec, bias_spec, wide_spec, wide_spec, square_spec, bias_spec),
        out_specs=(out_spec, out_spec),
        check_vma=False,
    )
```

profile of v0, /device:TPU:97, one launch (start us, length us, event | category | flops | bytes accessed | tf_op | source)
XLA Modules:
  0.0 6826.4 jit_solution(7151569044646041200)
XLA Ops:
  36.2 3400.8 %while.32 = (s32[]{:T(128)}, f32[32,1024]{1,0:T(8,128)}, bf16[32,512]{1,0:T(8,128)(2,1)S(1)}, bf16[24,32,512]{2,1,0:T(8,128)(2,1)}, bf16[24,32,512]{2,1,0:T(8,12...) while((s32[]{:T(128)}, f32[32,1024]{1,0:T(8,128)}, ...), condition=%wide.region_3.4_spmd, body=%wide.region_0.3_spmd.sunk | while | flops 202178560 | bytes 22622956 | solution.py:46
  177.1 56.9 all-reduce.5.cloned.1.call-done
  318.9 56.9 all-reduce.5.cloned.1.call-done
  460.8 57.0 all-reduce.5.cloned.1.call-done
  744.5 56.9 all-reduce.5.cloned.1.call-done
  886.3 56.9 all-reduce.5.cloned.1.call-done
  1028.2 56.9 all-reduce.5.cloned.1.call-done
  1170.0 56.9 all-reduce.5.cloned.1.call-done
  1311.8 56.9 all-reduce.5.cloned.1.call-done
  1453.6 57.0 all-reduce.5.cloned.1.call-done
  1737.4 56.9 all-reduce.5.cloned.1.call-done
  1879.2 57.0 all-reduce.5.cloned.1.call-done
  2163.0 57.0 all-reduce.5.cloned.1.call-done
  2304.9 57.0 all-reduce.5.cloned.1.call-done
  2588.6 57.0 all-reduce.5.cloned.1.call-done
  2730.5 57.0 all-reduce.5.cloned.1.call-done
  2872.4 57.0 all-reduce.5.cloned.1.call-done
  3014.4 57.0 all-reduce.5.cloned.1.call-done
  3156.3 56.9 all-reduce.5.cloned.1.call-done
  3298.1 56.9 all-reduce.5.cloned.1.call-done
  3436.9 3381.6 %while.33 = (s32[]{:T(128)}, f32[32,1024]{1,0:T(8,128)}, bf16[32,512]{1,0:T(8,128)(2,1)}, bf16[24,32,128]{2,1,0:T(8,128)(2,1)}, bf16[24,32,512]{2,1,0:T(8,128)(2...) while((s32[]{:T(128)}, f32[32,1024]{1,0:T(8,128)}, ...), condition=%wide.region_7.8_spmd, body=%wide.region_4.7_spmd.sunk | while | flops 202178560 | bytes 28029828 | solution.py:46
  3441.1 56.9 all-reduce.9.cloned.1.call-done
  3722.9 56.9 all-reduce.9.cloned.1.call-done
  4004.7 56.9 all-reduce.9.cloned.1.call-done
  (1172 shorter events, 5557.0 us)
Async XLA Ops:
  177.0 126.9 %all-reduce.7.cloned.1.call-start = ((), (), s32[]{:S(2)}) async-start(), calls=%async_computation.2 | async-start | bytes 262144 | tf_op jit(solution)/shard_map/while/body/eval_jaxpr/psum | solution.py:36
  318.9 126.9 %all-reduce.7.cloned.1.call-start = ((), (), s32[]{:S(2)}) async-start(), calls=%async_computation.2 | async-start | bytes 262144 | tf_op jit(solution)/shard_map/while/body/eval_jaxpr/psum | solution.py:36
  460.7 127.0 %all-reduce.7.cloned.1.call-start = ((), (), s32[]{:S(2)}) async-start(), calls=%async_computation.2 | async-start | bytes 262144 | tf_op jit(solution)/shard_map/while/body/eval_jaxpr/psum | solution.py:36
  602.6 126.9 %all-reduce.7.cloned.1.call-start = ((), (), s32[]{:S(2)}) async-start(), calls=%async_computation.2 | async-start | bytes 262144 | tf_op jit(solution)/shard_map/while/body/eval_jaxpr/psum | solution.py:36
  744.5 126.9 %all-reduce.7.cloned.1.call-start = ((), (), s32[]{:S(2)}) async-start(), calls=%async_computation.2 | async-start | bytes 262144 | tf_op jit(solution)/shard_map/while/body/eval_jaxpr/psum | solution.py:36
  886.3 126.9 %all-reduce.7.cloned.1.call-start = ((), (), s32[]{:S(2)}) async-start(), calls=%async_computation.2 | async-start | bytes 262144 | tf_op jit(solution)/shard_map/while/body/eval_jaxpr/psum | solution.py:36
  1028.1 126.9 %all-reduce.7.cloned.1.call-start = ((), (), s32[]{:S(2)}) async-start(), calls=%async_computation.2 | async-start | bytes 262144 | tf_op jit(solution)/shard_map/while/body/eval_jaxpr/psum | solution.py:36
  1169.9 126.9 %all-reduce.7.cloned.1.call-start = ((), (), s32[]{:S(2)}) async-start(), calls=%async_computation.2 | async-start | bytes 262144 | tf_op jit(solution)/shard_map/while/body/eval_jaxpr/psum | solution.py:36
  1311.7 126.9 %all-reduce.7.cloned.1.call-start = ((), (), s32[]{:S(2)}) async-start(), calls=%async_computation.2 | async-start | bytes 262144 | tf_op jit(solution)/shard_map/while/body/eval_jaxpr/psum | solution.py:36
  1453.6 127.0 %all-reduce.7.cloned.1.call-start = ((), (), s32[]{:S(2)}) async-start(), calls=%async_computation.2 | async-start | bytes 262144 | tf_op jit(solution)/shard_map/while/body/eval_jaxpr/psum | solution.py:36
  1595.5 126.9 %all-reduce.7.cloned.1.call-start = ((), (), s32[]{:S(2)}) async-start(), calls=%async_computation.2 | async-start | bytes 262144 | tf_op jit(solution)/shard_map/while/body/eval_jaxpr/psum | solution.py:36
  1737.3 126.9 %all-reduce.7.cloned.1.call-start = ((), (), s32[]{:S(2)}) async-start(), calls=%async_computation.2 | async-start | bytes 262144 | tf_op jit(solution)/shard_map/while/body/eval_jaxpr/psum | solution.py:36
  1879.1 127.0 %all-reduce.7.cloned.1.call-start = ((), (), s32[]{:S(2)}) async-start(), calls=%async_computation.2 | async-start | bytes 262144 | tf_op jit(solution)/shard_map/while/body/eval_jaxpr/psum | solution.py:36
  2021.1 126.9 %all-reduce.7.cloned.1.call-start = ((), (), s32[]{:S(2)}) async-start(), calls=%async_computation.2 | async-start | bytes 262144 | tf_op jit(solution)/shard_map/while/body/eval_jaxpr/psum | solution.py:36
  2162.9 127.0 %all-reduce.7.cloned.1.call-start = ((), (), s32[]{:S(2)}) async-start(), calls=%async_computation.2 | async-start | bytes 262144 | tf_op jit(solution)/shard_map/while/body/eval_jaxpr/psum | solution.py:36
  2304.8 127.0 %all-reduce.7.cloned.1.call-start = ((), (), s32[]{:S(2)}) async-start(), calls=%async_computation.2 | async-start | bytes 262144 | tf_op jit(solution)/shard_map/while/body/eval_jaxpr/psum | solution.py:36
  2446.7 126.9 %all-reduce.7.cloned.1.call-start = ((), (), s32[]{:S(2)}) async-start(), calls=%async_computation.2 | async-start | bytes 262144 | tf_op jit(solution)/shard_map/while/body/eval_jaxpr/psum | solution.py:36
  2588.5 127.0 %all-reduce.7.cloned.1.call-start = ((), (), s32[]{:S(2)}) async-start(), calls=%async_computation.2 | async-start | bytes 262144 | tf_op jit(solution)/shard_map/while/body/eval_jaxpr/psum | solution.py:36
  2730.5 127.0 %all-reduce.7.cloned.1.call-start = ((), (), s32[]{:S(2)}) async-start(), calls=%async_computation.2 | async-start | bytes 262144 | tf_op jit(solution)/shard_map/while/body/eval_jaxpr/psum | solution.py:36
  2872.4 127.0 %all-reduce.7.cloned.1.call-start = ((), (), s32[]{:S(2)}) async-start(), calls=%async_computation.2 | async-start | bytes 262144 | tf_op jit(solution)/shard_map/while/body/eval_jaxpr/psum | solution.py:36
  3014.3 127.0 %all-reduce.7.cloned.1.call-start = ((), (), s32[]{:S(2)}) async-start(), calls=%async_computation.2 | async-start | bytes 262144 | tf_op jit(solution)/shard_map/while/body/eval_jaxpr/psum | solution.py:36
  3156.2 126.9 %all-reduce.7.cloned.1.call-start = ((), (), s32[]{:S(2)}) async-start(), calls=%async_computation.2 | async-start | bytes 262144 | tf_op jit(solution)/shard_map/while/body/eval_jaxpr/psum | solution.py:36
  3298.0 126.9 %all-reduce.7.cloned.1.call-start = ((), (), s32[]{:S(2)}) async-start(), calls=%async_computation.2 | async-start | bytes 262144 | tf_op jit(solution)/shard_map/while/body/eval_jaxpr/psum | solution.py:36
  3581.9 124.8 %all-reduce.11.cloned.1.call-start = ((), (), s32[]{:S(2)}) async-start(), calls=%async_computation.4 | async-start | bytes 262144 | tf_op jit(solution)/shard_map/while/body/eval_jaxpr/psum | solution.py:36
  (244 other events, 10889.1 us)
Sparse Core Ops, SparseCore 0:
  177.2 56.7 all-reduce.4
  319.0 56.7 all-reduce.4
  460.9 56.7 all-reduce.4
  1453.8 56.7 all-reduce.4
  1879.4 56.7 all-reduce.4
  2163.1 56.7 all-reduce.4
  2305.0 56.7 all-reduce.4
  2588.8 56.7 all-reduce.4
  2730.7 56.7 all-reduce.4
  2872.6 56.7 all-reduce.4
  3014.5 56.7 all-reduce.4
  3298.2 56.7 all-reduce.4
  3441.2 56.7 all-reduce.8
  3723.0 56.7 all-reduce.8
  4004.8 56.7 all-reduce.8
  4286.6 56.7 all-reduce.8
  4568.4 56.7 all-reduce.8
  4850.2 56.7 all-reduce.8
  5132.0 56.7 all-reduce.8
  5413.8 56.7 all-reduce.8
  5695.6 56.7 all-reduce.8
  5977.4 56.7 all-reduce.8
  6259.2 56.7 all-reduce.8
  6541.0 56.7 all-reduce.8
  (73 shorter events, 4056.9 us)
where the time goes:
time: 6840 us; the launch traced here: 6830 us
  waiting for transfers between devices  5440 us (80%)
  blocking collectives  936 us (14%)
  matrix products  199 us (3%)
  other arithmetic  178 us (3%)
    psum x48, waiting for transfers between devices, gru_step(): gate_pre = lax.psum(part_sum, 'row') + gate_bias  2730 us
    psum x48, waiting for transfers between devices, gru_step(): lax.psum(jnp.dot(gated_row, w_hn, preferred_element_type=jnp.float32), 'r...  2690 us
    all_gather x96, blocking collectives, gather_rows(): gathered = lax.all_gather(col_part, 'col', axis=1, tiled=True)  936 us
  transfers between devices with their start and end apart: 97, of which 97 were waited for; matrix products, arithmetic and copies ran while one was open for 0% of the time, Pallas kernels for 0%

commit v1 on v0

v1 whole, which is shorter than its diff:
```python
import functools

import jax
import jax.numpy as jnp
from jax import lax
from jax.experimental import pallas as pl
from jax.experimental.pallas import tpu as pltpu
from jax.sharding import PartitionSpec as P

MESH = pl.DeviceIdType.MESH
F32 = jnp.float32
BF16 = jnp.bfloat16
HALVES = 2
CORES = 2
RESET, UPDATE, CAND, REC_RESET, REC_UPDATE, REC_CAND = range(6)
GATES = 6


def ring_distance(offset, count):
    return min(offset, count - offset)


def gru_kernel(
    rows, cols,
    x_ref, h_ref, wx1, wru1, wn1, b1, wx2, wru2, wn2, b2,
    seq_out, last_out,
    weights, relay, xs, x_relay, state_in,
    h1_blocks, r1_blocks, h2_blocks, r2_blocks,
    states, updates, projections, seq_halves, last_halves,
    weight_sem, relay_sem, xs_sem, x_relay_sem, state_sem,
    weight_sent, relay_sent, x_sent, x_relay_sent, state_sent,
    block_sem, block_sent, out_sem, out_sent,
):
    chips = rows // CORES
    steps, batch, half = seq_out.shape
    chunk = HALVES * half
    places = chips * cols
    row, col = lax.axis_index("row"), lax.axis_index("col")
    xpos, core = row // CORES, row % CORES
    layers = ((wx1, wru1, wn1), (wx2, wru2, wn2))

    def device(x, c, y):
        return {"row": CORES * x + c, "col": y}

    def wrap_x(v):
        return lax.rem(v + 2 * chips, chips)

    def wrap_y(v):
        return lax.rem(v + 2 * cols, cols)

    def place_of(x_from, y_from, x_to, y_to):
        return chips * wrap_y(y_from - y_to) + wrap_x(x_from - x_to)

    barrier = pltpu.get_barrier_semaphore()
    for k in range(1, rows * cols):
        other = {"row": lax.rem(row + k % rows, rows), "col": lax.rem(col + k // rows, cols)}
        pl.semaphore_signal(barrier, inc=1, device_id=other, device_id_type=MESH)
    pl.semaphore_wait(barrier, rows * cols - 1)

    def remote(src, dst, send, recv, to):
        return pltpu.make_async_remote_copy(
            src_ref=src, dst_ref=dst, send_sem=send, recv_sem=recv, device_id=to, device_id_type=MESH
        )

    def own_unit(j):
        return HALVES * core + j, xpos

    def weight_pieces(layer, j, x_to, dst):
        wx, wru, wn = layers[layer]
        depth = pl.ds(j * chunk, chunk)
        for s in range(HALVES):
            units = pl.ds(pl.multiple_of(x_to * chunk + s * half, half), half)
            yield wx.at[:, depth, units], dst.at[pl.ds(0, 3), s]
            yield wru.at[:, depth, units], dst.at[pl.ds(3, 2), s]
            yield wn.at[depth, units], dst.at[5, s]

    def x_pieces(j, dst):
        for s in range(HALVES):
            yield x_ref.at[:, :, pl.ds(j * chunk + s * half, half)], dst.at[:, s]

    def send_weights(layer):
        for j, turn in ((0, 1), (1, -1)):
            via, far = wrap_x(xpos + turn), wrap_x(xpos + 2)
            for src, dst in weight_pieces(layer, j, far, relay.at[layer, j, core]):
                remote(src, dst, weight_sent.at[layer, 2, j], relay_sem.at[layer, j, core], device(via, 0, col)).start()
        for turn in (1, chips - 1, 0):
            x_to = wrap_x(xpos + turn)
            for j in range(2):
                place = place_of(*own_unit(j), x_to, col)
                dst_chunk = weights.at[layer, place]

                def remote_pieces():
                    for src, dst in weight_pieces(layer, j, x_to, dst_chunk):
                        remote(src, dst, weight_sent.at[layer, turn, j], weight_sem.at[layer, place], device(x_to, 1, col)).start()

                if turn:
                    remote_pieces()
                else:
                    pl.when(core == 0)(remote_pieces)

                    @pl.when(core == 1)
                    def _():
                        for src, dst in weight_pieces(layer, j, x_to, dst_chunk):
                            pltpu.make_async_copy(src, dst, weight_sem.at[layer, place]).start()

    def send_x():
        for j, turn in ((0, 1), (1, -1)):
            via = wrap_x(xpos + turn)
            for src, dst in x_pieces(j, x_relay.at[j, core]):
                remote(src, dst, x_sent.at[2, j], x_relay_sem.at[j, core], device(via, 0, col)).start()
        for turn in (1, chips - 1, 0):
            x_to = wrap_x(xpos + turn)
            for j in range(2):
                place = place_of(*own_unit(j), x_to, col)

                def remote_pieces():
                    for src, dst in x_pieces(j, xs.at[place]):
                        remote(src, dst, x_sent.at[turn, j], xs_sem.at[place], device(x_to, 1, col)).start()

                if turn:
                    remote_pieces()
                else:
                    pl.when(core == 0)(remote_pieces)

                    @pl.when(core == 1)
                    def _():
                        for src, dst in x_pieces(j, xs.at[place]):
                            pltpu.make_async_copy(src, dst, xs_sem.at[place]).start()

    def pass_on(layer):
        for j, turn in ((0, 1), (1, -1)):
            for c in range(CORES):
                src = relay.at[layer, j, c]
                pltpu.make_async_copy(src, src, relay_sem.at[layer, j, c]).wait()
                x_to = wrap_x(xpos + turn)
                place = place_of(HALVES * c + j, wrap_x(xpos - turn), x_to, col)
                remote(src, weights.at[layer, place], relay_sent.at[layer, j, c], weight_sem.at[layer, place], device(x_to, 1, col)).start()

    def pass_on_x():
        for j, turn in ((0, 1), (1, -1)):
            for c in range(CORES):
                src = x_relay.at[j, c]
                pltpu.make_async_copy(src, src, x_relay_sem.at[j, c]).wait()
                x_to = wrap_x(xpos + turn)
                place = place_of(HALVES * c + j, wrap_x(xpos - turn), x_to, col)
                remote(src, xs.at[place], x_relay_sent.at[j, c], xs_sem.at[place], device(x_to, 1, col)).start()

    @pl.when(xpos == col)
    def _():
        for j in range(2):
            x_to = HALVES * core + j
            for s in range(HALVES):
                src = h_ref.at[:, :, pl.ds(j * chunk + s * half, half)]
                dst = state_in.at[:, s]
                mine = (x_to == xpos) & (core == 1)

                @pl.when(mine)
                def _():
                    pltpu.make_async_copy(src, dst, state_sem.at[s]).start()

                @pl.when(jnp.logical_not(mine))
                def _():
                    copy = remote(src, dst, state_sent.at[j, s], state_sem.at[s], device(x_to, 1, col))
                    copy.start()
                    copy.wait_send()

    send_weights(0)
    send_x()

    @pl.when(core == 0)
    def _():
        pass_on(0)
        pass_on_x()

    send_weights(1)

    @pl.when(core == 0)
    def _():
        pass_on(1)

    def drain_sends():
        piece = weights.at[0, 0]
        for layer in range(2):
            for j in range(2):
                for turn in (1, 2, chips - 1):
                    pltpu.make_async_copy(piece, piece, weight_sent.at[layer, turn, j]).wait()

                @pl.when(core == 0)
                def _():
                    pltpu.make_async_copy(piece, piece, weight_sent.at[layer, 0, j]).wait()
                    for c in range(CORES):
                        pltpu.make_async_copy(piece, piece, relay_sent.at[layer, j, c]).wait()

        part = xs.at[0]
        for j in range(2):
            for turn in (1, 2, chips - 1):
                pltpu.make_async_copy(part, part, x_sent.at[turn, j]).wait()

            @pl.when(core == 0)
            def _():
                pltpu.make_async_copy(part, part, x_sent.at[0, j]).wait()
                for c in range(CORES):
                    pltpu.make_async_copy(part, part, x_relay_sent.at[j, c]).wait()

    offsets = [(dx, dy) for dy in range(cols) for dx in range(chips)]
    distance = [ring_distance(dx, chips) + ring_distance(dy, cols) for dx, dy in offsets]
    far_first = sorted(range(1, places), key=lambda p: -distance[p])
    groups = [
        [p for p in range(places) if distance[p] <= 1],
        [p for p in range(places) if distance[p] == 2],
        [p for p in range(places) if distance[p] > 2],
    ]

    def spread(blocks, kind):
        for p in far_first:
            dx, dy = offsets[p]
            there = chips * ((cols - dy) % cols) + (chips - dx) % chips
            to = device(wrap_x(xpos + dx), 1, wrap_y(col + dy))
            remote(blocks.at[0], blocks.at[there], block_sent.at[kind], block_sem.at[kind, there], to).start()

    def arrived(blocks, kind, group):
        for p in group:
            if p:
                pltpu.make_async_copy(blocks.at[p], blocks.at[p], block_sem.at[kind, p]).wait()

    def all_sent(blocks, kind):
        sent = blocks.at[pl.ds(1, places - 1)]
        pltpu.make_async_copy(sent, sent, block_sent.at[kind]).wait()

    def wide(parts):
        return jnp.concatenate(parts, axis=1)

    def product(lhs_of, layer, gates, total=None, group=None):
        for p in range(places) if group is None else group:
            rhs = wide([weights[layer, p, g, s] for g in gates for s in range(HALVES)])
            lhs = wide([lhs_of(p, s) for s in range(HALVES)])
            term = jnp.dot(lhs, rhs, preferred_element_type=F32)
            total = term if total is None else total + term
        return total

    def gathered(blocks, kind, layer, gates):
        total = None
        for group in groups:
            arrived(blocks, kind, group)
            total = product(lambda p, s: blocks[p, s], layer, gates, total, group)
        return total

    def project(layer, lhs_of, bias):
        total = product(lhs_of, layer, (RESET, UPDATE, CAND))
        for g in range(3):
            for s in range(HALVES):
                n = g * HALVES + s
                here = bias[pl.ds(g, 1), pl.ds(pl.multiple_of(xpos * chunk + s * half, half), half)]
                projections[layer, g, s] = total[:, n * half : (n + 1) * half] + here

    def reset_half(layer, blocks, kind, out_blocks):
        total = gathered(blocks, kind, layer, (REC_RESET, REC_UPDATE))
        for s in range(HALVES):
            reset = jax.nn.sigmoid(projections[layer, RESET, s] + total[:, s * half : (s + 1) * half])
            out_blocks[0, s] = (reset * states[layer, s]).astype(BF16)
        for s in range(HALVES):
            n = HALVES + s
            updates[layer, s] = jax.nn.sigmoid(projections[layer, UPDATE, s] + total[:, n * half : (n + 1) * half])

    def next_half(layer, blocks, kind, emit):
        total = gathered(blocks, kind, layer, (REC_CAND,))
        for s in range(HALVES):
            candidate = jnp.tanh(projections[layer, CAND, s] + total[:, s * half : (s + 1) * half])
            update = updates[layer, s]
            state = (1.0 - update) * candidate + update * states[layer, s]
            states[layer, s] = state
            emit(s, state.astype(BF16))

    H1, R1, H2, R2 = range(4)

    def first_reset(t):
        slot = h1_blocks.at[lax.rem(t, 2)]
        reset_half(0, slot, H1, r1_blocks)
        all_sent(slot, H1)
        spread(r1_blocks, R1)

    def first_next(t):
        slot = h1_blocks.at[lax.rem(t + 1, 2)]

        def emit(s, value):
            slot[0, s] = value

        next_half(0, r1_blocks, R1, emit)
        all_sent(r1_blocks, R1)
        spread(slot, H1)

    def first_inputs(t):
        project(0, lambda p, s: xs[p, t, s], b1)

    def second_inputs(t):
        slot = h1_blocks.at[lax.rem(t, 2)]
        project(1, lambda p, s: slot[p, s], b2)

    def second_reset():
        reset_half(1, h2_blocks, H2, r2_blocks)
        all_sent(h2_blocks, H2)
        spread(r2_blocks, R2)

    def second_next(t, last):
        def emit(s, value):
            seq_halves[s, t] = value
            if not last:
                h2_blocks[0, s] = value

        next_half(1, r2_blocks, R2, emit)
        all_sent(r2_blocks, R2)
        if not last:
            spread(h2_blocks, H2)

    @pl.when(core == 1)
    def _():
        for s in range(HALVES):
            part = state_in.at[:, s]
            pltpu.make_async_copy(part, part, state_sem.at[s]).wait()
        for layer in range(2):
            for s in range(HALVES):
                states[layer, s] = state_in[layer, s]
        for s in range(HALVES):
            h1_blocks[0, 0, s] = state_in[0, s].astype(BF16)
            h2_blocks[0, s] = state_in[1, s].astype(BF16)
        spread(h1_blocks.at[0], H1)
        spread(h2_blocks, H2)
        for p in range(places):
            pltpu.make_async_copy(xs.at[p], xs.at[p], xs_sem.at[p]).wait()
            pltpu.make_async_copy(weights.at[0, p], weights.at[0, p], weight_sem.at[0, p]).wait()
        first_inputs(0)
        first_reset(0)
        first_next(0)
        first_inputs(jnp.minimum(1, steps - 1))
        for p in range(places):
            pltpu.make_async_copy(weights.at[1, p], weights.at[1, p], weight_sem.at[1, p]).wait()

        def step(t, carry):
            first_reset(t)
            second_inputs(t)
            second_reset()
            first_next(t)
            second_next(t - 1, False)
            first_inputs(jnp.minimum(t + 1, steps - 1))
            return carry

        lax.fori_loop(1, steps, step, 0)
        last_slot = h1_blocks.at[steps % 2]
        arrived(last_slot, H1, range(places))
        all_sent(last_slot, H1)
        second_inputs(steps)
        second_reset()
        second_next(steps - 1, True)
        for layer in range(2):
            for s in range(HALVES):
                last_halves[s, layer] = states[layer, s]
        seq_copy = remote(seq_halves.at[0], seq_out, out_sent.at[0], out_sem.at[0], device(xpos, 0, col))
        last_copy = remote(last_halves.at[0], last_out, out_sent.at[1], out_sem.at[1], device(xpos, 0, col))
        seq_copy.start()
        last_copy.start()
        seq_out[...] = seq_halves[1]
        last_out[...] = last_halves[1]
        seq_copy.wait_send()
        last_copy.wait_send()

    @pl.when(core == 0)
    def _():
        pltpu.make_async_copy(seq_out, seq_out, out_sem.at[0]).wait()
        pltpu.make_async_copy(last_out, last_out, out_sem.at[1]).wait()

    drain_sends()


def solution(mesh):
    rows, cols = mesh.shape["row"], mesh.shape["col"]
    chips = rows // CORES
    places = chips * cols

    def device_body(x_rows, h_rows, wx_l1, whru_l1, whn_l1, bias_l1, wx_l2, whru_l2, whn_l2, bias_l2):
        steps, batch, row_block = x_rows.shape
        col_block = wx_l1.shape[2]
        half = col_block // rows
        chunk = HALVES * half
        anywhere = pl.BlockSpec(memory_space=pl.ANY)
        vmem = pl.BlockSpec(memory_space=pltpu.VMEM)
        dma = pltpu.SemaphoreType.DMA
        kinds = 4
        block = (HALVES, batch, half)
        scratch = [
            pltpu.VMEM((2, places, GATES, HALVES, chunk, half), BF16),
            pltpu.VMEM((2, 2, CORES, GATES, HALVES, chunk, half), BF16),
            pltpu.VMEM((places, steps, *block), BF16),
            pltpu.VMEM((2, CORES, steps, *block), BF16),
            pltpu.VMEM((2, *block), F32),
            pltpu.VMEM((2, places, *block), BF16),
            pltpu.VMEM((places, *block), BF16),
            pltpu.VMEM((places, *block), BF16),
            pltpu.VMEM((places, *block), BF16),
            pltpu.VMEM((2, *block), F32),
            pltpu.VMEM((2, *block), F32),
            pltpu.VMEM((2, 3, *block), F32),
            pltpu.VMEM((HALVES, steps, batch, half), BF16),
            pltpu.VMEM((HALVES, 2, batch, half), F32),
            dma((2, places)),
            dma((2, 2, CORES)),
            dma((places,)),
            dma((2, CORES)),
            dma((HALVES,)),
            dma((2, chips, 2)),
            dma((2, 2, CORES)),
            dma((chips, 2)),
            dma((2, CORES)),
            dma((2, HALVES)),
            dma((kinds, places)),
            dma((kinds,)),
            dma((2,)),
            dma((2,)),
        ]
        return pl.pallas_call(
            functools.partial(gru_kernel, rows, cols),
            name="gru",
            out_shape=(
                jax.ShapeDtypeStruct((steps, batch, half), BF16),
                jax.ShapeDtypeStruct((2, batch, half), F32),
            ),
            in_specs=[anywhere, anywhere, anywhere, anywhere, anywhere, vmem, anywhere, anywhere, anywhere, vmem],
            out_specs=(vmem, vmem),
            scratch_shapes=scratch,
            compiler_params=pltpu.CompilerParams(
                collective_id=0, has_side_effects=True, vmem_limit_bytes=60 * 1024 * 1024
            ),
        )(
            x_rows, h_rows,
            jnp.transpose(wx_l1, (1, 0, 2)), jnp.transpose(whru_l1, (1, 0, 2)), whn_l1, bias_l1,
            jnp.transpose(wx_l2, (1, 0, 2)), jnp.transpose(whru_l2, (1, 0, 2)), whn_l2, bias_l2,
        )

    seq_spec = P(None, "data", "row")
    out_spec = P(None, "data", ("col", "row"))
    wide_spec = P("row", None, "col")
    square_spec = P("row", "col")
    bias_spec = P(None, "col")
    return jax.shard_map(
        device_body,
        mesh=mesh,
        in_specs=(seq_spec, seq_spec, wide_spec, wide_spec, square_spec, bias_spec, wide_spec, wide_spec, square_spec, bias_spec),
        out_specs=(out_spec, out_spec),
        check_vma=False,
    )
```

time: 6840 us -> 467 us (0.07)
  waiting for transfers between devices: 5440 us -> 0 us
  blocking collectives: 936 us -> 0 us
  Pallas kernels: 0 us -> 457 us
  matrix products: 199 us -> 0 us
  other arithmetic: 178 us -> 0 us
    psum x96 -> x0, waiting for transfers between devices: 5410 us -> none  [the longest x48 2730 us: gru_step(): gate_pre = lax.psum(part_sum, 'row') + gate_bias]
    all_gather x96 -> x0, blocking collectives: 936 us -> none  [gather_rows(): gathered = lax.all_gather(col_part, 'col', axis=1, tiled=True)]
    pallas_call x0 -> x1, Pallas kernels: none -> 457 us  [device_body(): pl.pallas_call(functools.partial(gru_kernel, rows, cols), name='gru', out...]
    dot_general x144 -> x0, matrix products: 199 us -> none  [the longest x48 102 us: gru_step(): jnp.einsum('bk,kgn->bgn', step_in, w_x, preferred_element_type=jnp.float32)]
    convert_element_type x97 -> x0, other arithmetic: 89.5 us -> none  [the longest x48 64.6 us: gru_step(): next_row = gather_rows(h_next.astype(jnp.bfloat16), row_idx, row_block)]
  transfers between devices with their start and end apart: 97 -> 0, of which waited for: 97 -> 0; matrix products, arithmetic and copies ran while one was open for 0% -> 0% of each run, Pallas kernels for 0% -> 0%
where the time goes in v1:
time: 467 us; the launch traced here: 466 us
  Pallas kernels  457 us (98%)
  local copies, waits for them, and re-layouts  8.46 us (2%)
    pallas_call x1, Pallas kernels, device_body(): pl.pallas_call(functools.partial(gru_kernel, rows, cols), name='gru', out...  457 us

profile of v1, /device:TPU:97, one launch (start us, length us, event | category | flops | bytes accessed | tf_op | source)
XLA Modules:
  0.0 466.4 jit_solution(15325007749368017412)
XLA Ops:
  0.6 5.5 %copy_bitcast_fusion = (bf16[2,512,1024]{2,1,0:T(8,128)(2,1)}, bf16[2,512,1024]{2,1,0:T(8,128)(2,1)}) fusion(bf16[512,2,1024]{2,1,0:T(2,128)(2,1)} %param.17, bf16[512,2,1024]{2,1,0:T(2,128)(2,1)} %param.13), kind=kLoop, calls=%fused_computation | loop fusion | bytes 8388608 | tf_op jit(solution)/shard_map/transpose | solution.py:435
  6.1 457.3 %gru.1 = (bf16[24,32,128]{2,1,0:T(8,128)(2,1)}, f32[2,32,128]{2,1,0:T(8,128)}) custom-call(bf16[24,32,512]{2,1,0:T(8,128)(2,1)} %x_ref.1, f32[2,32,512]{2,1,0:T(8,128)} %h_ref.1, bf16[3,512,1024]{2,1,0:T(8,128)(2,1)} %bitcast.6, bf16[2,512,1024]{2,1,0:T(8,128)(2,1)} %get-tuple-element.3.wru1, bf16[512,1024]{1,0:T(8,128)(2,1)} %wn1.1, f32[3,1024]{1,0:T(4,128)} %b1.1, ...), custom_call_target="tpu_custom_call" | custom-call | tf_op jit(solution)/shard_map/gru/pallas_call | solution.py:419
  463.5 1.6 copy.18
  465.1 1.4 copy.19

commit v2 on v1

--- a/solution.py
+++ b/solution.py
@@ -24,11 +24,11 @@
     rows, cols,
     x_ref, h_ref, wx1, wru1, wn1, b1, wx2, wru2, wn2, b2,
     seq_out, last_out,
-    weights, relay, xs, x_relay, state_in,
+    weights, xs, state_in,
     h1_blocks, r1_blocks, h2_blocks, r2_blocks,
     states, updates, projections, seq_halves, last_halves,
-    weight_sem, relay_sem, xs_sem, x_relay_sem, state_sem,
-    weight_sent, relay_sent, x_sent, x_relay_sent, state_sent,
+    weight_sem, hand_sem, x_sem, xs_sem, state_sem,
+    weight_sent, handed_sent, x_sent, x_passed, state_sent,
     block_sem, block_sent, out_sem, out_sent,
 ):
     chips = rows // CORES
@@ -62,8 +62,8 @@
             src_ref=src, dst_ref=dst, send_sem=send, recv_sem=recv, device_id=to, device_id_type=MESH
         )
 
-    def own_unit(j):
-        return HALVES * core + j, xpos
+    def chunk_place(c, j, x_from, x_to, y_to):
+        return place_of(HALVES * c + j, x_from, x_to, y_to)
 
     def weight_pieces(layer, j, x_to, dst):
         wx, wru, wn = layers[layer]
@@ -74,76 +74,68 @@
             yield wru.at[:, depth, units], dst.at[pl.ds(3, 2), s]
             yield wn.at[depth, units], dst.at[5, s]
 
+    def send_weights(layer, turns):
+        for turn in turns:
+            x_to = wrap_x(xpos + turn)
+            for j in range(2):
+                place = chunk_place(core, j, xpos, x_to, col)
+                for src, dst in weight_pieces(layer, j, x_to, weights.at[layer, place]):
+                    remote(src, dst, weight_sent.at[layer, turn, j], weight_sem.at[layer, place], device(x_to, 1, col)).start()
+
+    def keep_weights(layer):
+        for j in range(2):
+            place = chunk_place(1, j, xpos, xpos, col)
+            for src, dst in weight_pieces(layer, j, xpos, weights.at[layer, place]):
+                pltpu.make_async_copy(src, dst, weight_sem.at[layer, place]).start()
+
+    def hand_over():
+        for turn in far_turns:
+            x_to = wrap_x(xpos + turn)
+            for j in range(2):
+                for src, dst in weight_pieces(1, j, x_to, weights.at[1, 2 * turn + j]):
+                    remote(src, dst, weight_sent.at[1, turn, j], hand_sem.at[turn, j], device(xpos, 0, col)).start()
+
+    def send_handed():
+        for turn in far_turns:
+            x_to = wrap_x(xpos + turn)
+            for j in range(2):
+                src = weights.at[1, 2 * turn + j]
+                pltpu.make_async_copy(src, src, hand_sem.at[turn, j]).wait()
+                place = chunk_place(1, j, xpos, x_to, col)
+                remote(src, weights.at[1, place], handed_sent.at[turn, j], weight_sem.at[1, place], device(x_to, 1, col)).start()
+
+    share = steps // cols
+    my_share = pl.ds(pl.multiple_of(col * share, share), share)
+
     def x_pieces(j, dst):
         for s in range(HALVES):
-            yield x_ref.at[:, :, pl.ds(j * chunk + s * half, half)], dst.at[:, s]
-
-    def send_weights(layer):
-        for j, turn in ((0, 1), (1, -1)):
-            via, far = wrap_x(xpos + turn), wrap_x(xpos + 2)
-            for src, dst in weight_pieces(layer, j, far, relay.at[layer, j, core]):
-                remote(src, dst, weight_sent.at[layer, 2, j], relay_sem.at[layer, j, core], device(via, 0, col)).start()
-        for turn in (1, chips - 1, 0):
+            yield x_ref.at[my_share, :, pl.ds(j * chunk + s * half, half)], dst.at[my_share, s]
+
+    def send_x(turns):
+        for turn in turns:
             x_to = wrap_x(xpos + turn)
             for j in range(2):
-                place = place_of(*own_unit(j), x_to, col)
-                dst_chunk = weights.at[layer, place]
-
-                def remote_pieces():
-                    for src, dst in weight_pieces(layer, j, x_to, dst_chunk):
-                        remote(src, dst, weight_sent.at[layer, turn, j], weight_sem.at[layer, place], device(x_to, 1, col)).start()
-
-                if turn:
-                    remote_pieces()
-                else:
-                    pl.when(core == 0)(remote_pieces)
-
-                    @pl.when(core == 1)
-                    def _():
-                        for src, dst in weight_pieces(layer, j, x_to, dst_chunk):
-                            pltpu.make_async_copy(src, dst, weight_sem.at[layer, place]).start()
-
-    def send_x():
-        for j, turn in ((0, 1), (1, -1)):
-            via = wrap_x(xpos + turn)
-            for src, dst in x_pieces(j, x_relay.at[j, core]):
-                remote(src, dst, x_sent.at[2, j], x_relay_sem.at[j, core], device(via, 0, col)).start()
-        for turn in (1, chips - 1, 0):
-            x_to = wrap_x(xpos + turn)
-            for j in range(2):
-                place = place_of(*own_unit(j), x_to, col)
-
-                def remote_pieces():
-                    for src, dst in x_pieces(j, xs.at[place]):
-                        remote(src, dst, x_sent.at[turn, j], xs_sem.at[place], device(x_to, 1, col)).start()
-
-                if turn:
-                    remote_pieces()
-                else:
-                    pl.when(core == 0)(remote_pieces)
-
-                    @pl.when(core == 1)
-                    def _():
-                        for src, dst in x_pieces(j, xs.at[place]):
-                            pltpu.make_async_copy(src, dst, xs_sem.at[place]).start()
-
-    def pass_on(layer):
-        for j, turn in ((0, 1), (1, -1)):
-            for c in range(CORES):
-                src = relay.at[layer, j, c]
-                pltpu.make_async_copy(src, src, relay_sem.at[layer, j, c]).wait()
-                x_to = wrap_x(xpos + turn)
-                place = place_of(HALVES * c + j, wrap_x(xpos - turn), x_to, col)
-                remote(src, weights.at[layer, place], relay_sent.at[layer, j, c], weight_sem.at[layer, place], device(x_to, 1, col)).start()
-
-    def pass_on_x():
-        for j, turn in ((0, 1), (1, -1)):
-            for c in range(CORES):
-                src = x_relay.at[j, c]
-                pltpu.make_async_copy(src, src, x_relay_sem.at[j, c]).wait()
-                x_to = wrap_x(xpos + turn)
-                place = place_of(HALVES * c + j, wrap_x(xpos - turn), x_to, col)
-                remote(src, xs.at[place], x_relay_sent.at[j, c], xs_sem.at[place], device(x_to, 1, col)).start()
+                place = chunk_place(core, j, xpos, x_to, col)
+                for src, dst in x_pieces(j, xs.at[place]):
+                    remote(src, dst, x_sent.at[turn, j], x_sem.at[place], device(x_to, 0, col)).start()
+
+    def keep_x():
+        for j in range(2):
+            place = chunk_place(0, j, xpos, xpos, col)
+            for src, dst in x_pieces(j, xs.at[place]):
+                pltpu.make_async_copy(src, dst, x_sem.at[place]).start()
+
+    def pass_x_on():
+        for p in range(places):
+            part = xs.at[p, my_share]
+            pltpu.make_async_copy(part, part, x_sem.at[p]).wait()
+        for k in range(cols):
+            for dy in range(cols):
+                src = xs.at[pl.ds(chips * dy, chips), my_share]
+                dst = xs.at[pl.ds(chips * ((dy - k) % cols), chips), my_share]
+                remote(src, dst, x_passed.at[k], xs_sem.at[col], device(xpos, 1, wrap_y(col + k))).start()
+
+    far_turns = (2, 1, chips - 1)
 
     @pl.when(xpos == col)
     def _():
@@ -164,43 +156,53 @@
                     copy.start()
                     copy.wait_send()
 
-    send_weights(0)
-    send_x()
+    send_x(far_turns)
+    pl.when(core == 1)(lambda: send_x((0,)))
+    pl.when(core == 0)(keep_x)
+    send_weights(0, far_turns)
+
+    @pl.when(core == 1)
+    def _():
+        keep_weights(0)
+        hand_over()
+        keep_weights(1)
 
     @pl.when(core == 0)
     def _():
-        pass_on(0)
-        pass_on_x()
-
-    send_weights(1)
-
-    @pl.when(core == 0)
-    def _():
-        pass_on(1)
+        send_weights(0, (0,))
+        pass_x_on()
+        send_weights(1, far_turns)
+        send_weights(1, (0,))
+        send_handed()
 
     def drain_sends():
         piece = weights.at[0, 0]
         for layer in range(2):
             for j in range(2):
-                for turn in (1, 2, chips - 1):
+                for turn in far_turns:
                     pltpu.make_async_copy(piece, piece, weight_sent.at[layer, turn, j]).wait()
 
                 @pl.when(core == 0)
                 def _():
                     pltpu.make_async_copy(piece, piece, weight_sent.at[layer, 0, j]).wait()
-                    for c in range(CORES):
-                        pltpu.make_async_copy(piece, piece, relay_sent.at[layer, j, c]).wait()
-
-        part = xs.at[0]
+        part = xs.at[0, my_share]
         for j in range(2):
-            for turn in (1, 2, chips - 1):
+            for turn in far_turns:
                 pltpu.make_async_copy(part, part, x_sent.at[turn, j]).wait()
 
-            @pl.when(core == 0)
-            def _():
+        @pl.when(core == 0)
+        def _():
+            for j in range(2):
+                for turn in far_turns:
+                    pltpu.make_async_copy(piece, piece, handed_sent.at[turn, j]).wait()
+            whole = xs.at[:, my_share]
+            for k in range(cols):
+                pltpu.make_async_copy(whole, whole, x_passed.at[k]).wait()
+
+        @pl.when(core == 1)
+        def _():
+            for j in range(2):
                 pltpu.make_async_copy(part, part, x_sent.at[0, j]).wait()
-                for c in range(CORES):
-                    pltpu.make_async_copy(part, part, x_relay_sent.at[j, c]).wait()
 
     offsets = [(dx, dy) for dy in range(cols) for dx in range(chips)]
     distance = [ring_distance(dx, chips) + ring_distance(dy, cols) for dx, dy in offsets]
@@ -253,11 +255,12 @@
                 here = bias[pl.ds(g, 1), pl.ds(pl.multiple_of(xpos * chunk + s * half, half), half)]
                 projections[layer, g, s] = total[:, n * half : (n + 1) * half] + here
 
-    def reset_half(layer, blocks, kind, out_blocks):
+    def reset_half(layer, blocks, kind, out_blocks, send):
         total = gathered(blocks, kind, layer, (REC_RESET, REC_UPDATE))
         for s in range(HALVES):
             reset = jax.nn.sigmoid(projections[layer, RESET, s] + total[:, s * half : (s + 1) * half])
             out_blocks[0, s] = (reset * states[layer, s]).astype(BF16)
+        send()
         for s in range(HALVES):
             n = HALVES + s
             updates[layer, s] = jax.nn.sigmoid(projections[layer, UPDATE, s] + total[:, n * half : (n + 1) * half])
@@ -275,9 +278,8 @@
 
     def first_reset(t):
         slot = h1_blocks.at[lax.rem(t, 2)]
-        reset_half(0, slot, H1, r1_blocks)
+        reset_half(0, slot, H1, r1_blocks, lambda: spread(r1_blocks, R1))
         all_sent(slot, H1)
-        spread(r1_blocks, R1)
 
     def first_next(t):
         slot = h1_blocks.at[lax.rem(t + 1, 2)]
@@ -297,9 +299,8 @@
         project(1, lambda p, s: slot[p, s], b2)
 
     def second_reset():
-        reset_half(1, h2_blocks, H2, r2_blocks)
+        reset_half(1, h2_blocks, H2, r2_blocks, lambda: spread(r2_blocks, R2))
         all_sent(h2_blocks, H2)
-        spread(r2_blocks, R2)
 
     def second_next(t, last):
         def emit(s, value):
@@ -325,8 +326,10 @@
             h2_blocks[0, s] = state_in[1, s].astype(BF16)
         spread(h1_blocks.at[0], H1)
         spread(h2_blocks, H2)
+        for y in range(cols):
+            part = xs.at[:, pl.ds(y * share, share)]
+            pltpu.make_async_copy(part, part, xs_sem.at[y]).wait()
         for p in range(places):
-            pltpu.make_async_copy(xs.at[p], xs.at[p], xs_sem.at[p]).wait()
             pltpu.make_async_copy(weights.at[0, p], weights.at[0, p], weight_sem.at[0, p]).wait()
         first_inputs(0)
         first_reset(0)
@@ -388,9 +391,7 @@
         block = (HALVES, batch, half)
         scratch = [
             pltpu.VMEM((2, places, GATES, HALVES, chunk, half), BF16),
-            pltpu.VMEM((2, 2, CORES, GATES, HALVES, chunk, half), BF16),
             pltpu.VMEM((places, steps, *block), BF16),
-            pltpu.VMEM((2, CORES, steps, *block), BF16),
             pltpu.VMEM((2, *block), F32),
             pltpu.VMEM((2, places, *block), BF16),
             pltpu.VMEM((places, *block), BF16),
@@ -402,14 +403,14 @@
             pltpu.VMEM((HALVES, steps, batch, half), BF16),
             pltpu.VMEM((HALVES, 2, batch, half), F32),
             dma((2, places)),
-            dma((2, 2, CORES)),
+            dma((chips, 2)),
             dma((places,)),
-            dma((2, CORES)),
+            dma((cols,)),
             dma((HALVES,)),
             dma((2, chips, 2)),
-            dma((2, 2, CORES)),
             dma((chips, 2)),
-            dma((2, CORES)),
+            dma((chips, 2)),
+            dma((cols,)),
             dma((2, HALVES)),
             dma((kinds, places)),
             dma((kinds,)),

time: 467 us -> 443 us (0.949)
  Pallas kernels: 457 us -> 433 us
    pallas_call x1, Pallas kernels: 457 us -> 433 us  [device_body(): pl.pallas_call(functools.partial(gru_kernel, rows, cols), name='gru', out...]
where the time goes in v2:
time: 443 us; the launch traced here: 442 us
  Pallas kernels  433 us (98%)
  local copies, waits for them, and re-layouts  8.46 us (2%)
    pallas_call x1, Pallas kernels, device_body(): pl.pallas_call(functools.partial(gru_kernel, rows, cols), name='gru', out...  433 us

profile of v2, /device:TPU:97, one launch (start us, length us, event | category | flops | bytes accessed | tf_op | source)
XLA Modules:
  0.0 442.5 jit_solution(12791820947419323626)
XLA Ops:
  0.6 5.5 %copy_bitcast_fusion = (bf16[2,512,1024]{2,1,0:T(8,128)(2,1)}, bf16[2,512,1024]{2,1,0:T(8,128)(2,1)}) fusion(bf16[512,2,1024]{2,1,0:T(2,128)(2,1)} %param.17, bf16[512,2,1024]{2,1,0:T(2,128)(2,1)} %param.13), kind=kLoop, calls=%fused_computation | loop fusion | bytes 8388608 | tf_op jit(solution)/shard_map/transpose | solution.py:436
  6.1 433.4 %gru.1 = (bf16[24,32,128]{2,1,0:T(8,128)(2,1)}, f32[2,32,128]{2,1,0:T(8,128)}) custom-call(bf16[24,32,512]{2,1,0:T(8,128)(2,1)} %x_ref.1, f32[2,32,512]{2,1,0:T(8,128)} %h_ref.1, bf16[3,512,1024]{2,1,0:T(8,128)(2,1)} %bitcast.6, bf16[2,512,1024]{2,1,0:T(8,128)(2,1)} %get-tuple-element.3.wru1, bf16[512,1024]{1,0:T(8,128)(2,1)} %wn1.1, f32[3,1024]{1,0:T(4,128)} %b1.1, ...), custom_call_target="tpu_custom_call" | custom-call | tf_op jit(solution)/shard_map/gru/pallas_call | solution.py:420
  439.5 1.6 copy.18
  441.1 1.4 copy.19

commit v3 on v2

--- a/solution.py
+++ b/solution.py
@@ -207,11 +207,7 @@
     offsets = [(dx, dy) for dy in range(cols) for dx in range(chips)]
     distance = [ring_distance(dx, chips) + ring_distance(dy, cols) for dx, dy in offsets]
     far_first = sorted(range(1, places), key=lambda p: -distance[p])
-    groups = [
-        [p for p in range(places) if distance[p] <= 1],
-        [p for p in range(places) if distance[p] == 2],
-        [p for p in range(places) if distance[p] > 2],
-    ]
+    by_arrival = sorted(range(places), key=lambda p: (distance[p], ring_distance(offsets[p][0], chips)))
 
     def spread(blocks, kind):
         for p in far_first:
@@ -220,10 +216,8 @@
             to = device(wrap_x(xpos + dx), 1, wrap_y(col + dy))
             remote(blocks.at[0], blocks.at[there], block_sent.at[kind], block_sem.at[kind, there], to).start()
 
-    def arrived(blocks, kind, group):
-        for p in group:
-            if p:
-                pltpu.make_async_copy(blocks.at[p], blocks.at[p], block_sem.at[kind, p]).wait()
+    def arrived(blocks, kind, p):
+        pltpu.make_async_copy(blocks.at[p], blocks.at[p], block_sem.at[kind, p]).wait()
 
     def all_sent(blocks, kind):
         sent = blocks.at[pl.ds(1, places - 1)]
@@ -232,23 +226,22 @@
     def wide(parts):
         return jnp.concatenate(parts, axis=1)
 
-    def product(lhs_of, layer, gates, total=None, group=None):
-        for p in range(places) if group is None else group:
+    def product(lhs_of, layer, gates, order, before=None):
+        total = None
+        for p in order:
+            if before is not None and p:
+                before(p)
             rhs = wide([weights[layer, p, g, s] for g in gates for s in range(HALVES)])
             lhs = wide([lhs_of(p, s) for s in range(HALVES)])
             term = jnp.dot(lhs, rhs, preferred_element_type=F32)
             total = term if total is None else total + term
         return total
 
-    def gathered(blocks, kind, layer, gates):
-        total = None
-        for group in groups:
-            arrived(blocks, kind, group)
-            total = product(lambda p, s: blocks[p, s], layer, gates, total, group)
-        return total
+    def gathered(blocks, kind, layer, gate):
+        return product(lambda p, s: blocks[p, s], layer, (gate,), by_arrival, lambda p: arrived(blocks, kind, p))
 
     def project(layer, lhs_of, bias):
-        total = product(lhs_of, layer, (RESET, UPDATE, CAND))
+        total = product(lhs_of, layer, (RESET, UPDATE, CAND), range(places))
         for g in range(3):
             for s in range(HALVES):
                 n = g * HALVES + s
@@ -256,23 +249,23 @@
                 projections[layer, g, s] = total[:, n * half : (n + 1) * half] + here
 
     def reset_half(layer, blocks, kind, out_blocks, send):
-        total = gathered(blocks, kind, layer, (REC_RESET, REC_UPDATE))
+        total = gathered(blocks, kind, layer, REC_RESET)
         for s in range(HALVES):
             reset = jax.nn.sigmoid(projections[layer, RESET, s] + total[:, s * half : (s + 1) * half])
             out_blocks[0, s] = (reset * states[layer, s]).astype(BF16)
         send()
-        for s in range(HALVES):
-            n = HALVES + s
-            updates[layer, s] = jax.nn.sigmoid(projections[layer, UPDATE, s] + total[:, n * half : (n + 1) * half])
+        total = product(lambda p, s: blocks[p, s], layer, (REC_UPDATE,), range(places))
+        for s in range(HALVES):
+            updates[layer, s] = jax.nn.sigmoid(projections[layer, UPDATE, s] + total[:, s * half : (s + 1) * half])
 
     def next_half(layer, blocks, kind, emit):
-        total = gathered(blocks, kind, layer, (REC_CAND,))
+        total = gathered(blocks, kind, layer, REC_CAND)
         for s in range(HALVES):
             candidate = jnp.tanh(projections[layer, CAND, s] + total[:, s * half : (s + 1) * half])
             update = updates[layer, s]
             state = (1.0 - update) * candidate + update * states[layer, s]
+            emit(s, state.astype(BF16))
             states[layer, s] = state
-            emit(s, state.astype(BF16))
 
     H1, R1, H2, R2 = range(4)
 
@@ -298,20 +291,23 @@
         slot = h1_blocks.at[lax.rem(t, 2)]
         project(1, lambda p, s: slot[p, s], b2)
 
-    def second_reset():
-        reset_half(1, h2_blocks, H2, r2_blocks, lambda: spread(r2_blocks, R2))
-        all_sent(h2_blocks, H2)
+    def second_reset(t):
+        slot = h2_blocks.at[lax.rem(t, 2)]
+        reset_half(1, slot, H2, r2_blocks, lambda: spread(r2_blocks, R2))
+        all_sent(slot, H2)
 
     def second_next(t, last):
+        slot = h2_blocks.at[lax.rem(t + 1, 2)]
+
         def emit(s, value):
             seq_halves[s, t] = value
             if not last:
-                h2_blocks[0, s] = value
+                slot[0, s] = value
 
         next_half(1, r2_blocks, R2, emit)
         all_sent(r2_blocks, R2)
         if not last:
-            spread(h2_blocks, H2)
+            spread(slot, H2)
 
     @pl.when(core == 1)
     def _():
@@ -323,9 +319,9 @@
                 states[layer, s] = state_in[layer, s]
         for s in range(HALVES):
             h1_blocks[0, 0, s] = state_in[0, s].astype(BF16)
-            h2_blocks[0, s] = state_in[1, s].astype(BF16)
+            h2_blocks[0, 0, s] = state_in[1, s].astype(BF16)
         spread(h1_blocks.at[0], H1)
-        spread(h2_blocks, H2)
+        spread(h2_blocks.at[0], H2)
         for y in range(cols):
             part = xs.at[:, pl.ds(y * share, share)]
             pltpu.make_async_copy(part, part, xs_sem.at[y]).wait()
@@ -341,7 +337,7 @@
         def step(t, carry):
             first_reset(t)
             second_inputs(t)
-            second_reset()
+            second_reset(t - 1)
             first_next(t)
             second_next(t - 1, False)
             first_inputs(jnp.minimum(t + 1, steps - 1))
@@ -349,10 +345,11 @@
 
         lax.fori_loop(1, steps, step, 0)
         last_slot = h1_blocks.at[steps % 2]
-        arrived(last_slot, H1, range(places))
+        for p in range(1, places):
+            arrived(last_slot, H1, p)
         all_sent(last_slot, H1)
         second_inputs(steps)
-        second_reset()
+        second_reset(steps - 1)
         second_next(steps - 1, True)
         for layer in range(2):
             for s in range(HALVES):
@@ -395,7 +392,7 @@
             pltpu.VMEM((2, *block), F32),
             pltpu.VMEM((2, places, *block), BF16),
             pltpu.VMEM((places, *block), BF16),
-            pltpu.VMEM((places, *block), BF16),
+            pltpu.VMEM((2, places, *block), BF16),
             pltpu.VMEM((places, *block), BF16),
             pltpu.VMEM((2, *block), F32),
             pltpu.VMEM((2, *block), F32),

time: 443 us -> 435 us (0.982)
  Pallas kernels: 433 us -> 426 us
    pallas_call x1, Pallas kernels: 433 us -> 426 us  [device_body(): pl.pallas_call(functools.partial(gru_kernel, rows, cols), name='gru', out...]
where the time goes in v3:
time: 435 us
  Pallas kernels  426 us (98%)
  local copies, waits for them, and re-layouts  8.46 us (2%)
    pallas_call x1, Pallas kernels, device_body(): pl.pallas_call(functools.partial(gru_kernel, rows, cols), name='gru', out...  426 us

profile of v3, /device:TPU:97, one launch (start us, length us, event | category | flops | bytes accessed | tf_op | source)
XLA Modules:
  0.0 434.6 jit_solution(9911803307508899504)
XLA Ops:
  0.6 5.5 %copy_bitcast_fusion = (bf16[2,512,1024]{2,1,0:T(8,128)(2,1)}, bf16[2,512,1024]{2,1,0:T(8,128)(2,1)}) fusion(bf16[512,2,1024]{2,1,0:T(2,128)(2,1)} %param.17, bf16[512,2,1024]{2,1,0:T(2,128)(2,1)} %param.13), kind=kLoop, calls=%fused_computation | loop fusion | bytes 8388608 | tf_op jit(solution)/shard_map/transpose | solution.py:433
  6.1 425.5 %gru.1 = (bf16[24,32,128]{2,1,0:T(8,128)(2,1)}, f32[2,32,128]{2,1,0:T(8,128)}) custom-call(bf16[24,32,512]{2,1,0:T(8,128)(2,1)} %x_ref.1, f32[2,32,512]{2,1,0:T(8,128)} %h_ref.1, bf16[3,512,1024]{2,1,0:T(8,128)(2,1)} %bitcast.6, bf16[2,512,1024]{2,1,0:T(8,128)(2,1)} %get-tuple-element.3.wru1, bf16[512,1024]{1,0:T(8,128)(2,1)} %wn1.1, f32[3,1024]{1,0:T(4,128)} %b1.1, ...), custom_call_target="tpu_custom_call" | custom-call | tf_op jit(solution)/shard_map/gru/pallas_call | solution.py:417
  431.6 1.6 copy.18
  433.2 1.4 copy.19

commit v4 on v3

v4 whole, which is shorter than its diff:
```python
import functools

import jax
import jax.numpy as jnp
from jax import lax
from jax.experimental import pallas as pl
from jax.experimental.pallas import tpu as pltpu
from jax.sharding import PartitionSpec as P

MESH = pl.DeviceIdType.MESH
F32 = jnp.float32
BF16 = jnp.bfloat16
HALVES = 2
CORES = 2
RESET, UPDATE, CAND = range(3)
GATES = 3


def ring_distance(offset, count):
    return min(offset, count - offset)


def gru_kernel(
    rows, cols,
    x_ref, h_ref, wx1, wru1, wn1, b1, wx2, wru2, wn2, b2,
    seq_out, last_out,
    recurrent, inputs, xs, state_in, h1_here,
    h1_blocks, r1_blocks, h2_blocks, r2_blocks,
    first_p, second_p, first_made, second_made,
    states, updates, seq_halves, last_halves,
    recurrent_sem, inputs_sem, hand_sem, x_sem, xs_sem, state_sem,
    recurrent_sent, inputs_sent, handed_sent, x_sent, x_passed, state_sent,
    block_sem, block_sent, h1_sem, h1_sent, first_sem, first_sent, second_sem, second_sent,
    out_sem, out_sent,
):
    chips = rows // CORES
    steps, batch, half = seq_out.shape
    chunk = HALVES * half
    places = chips * cols
    row, col = lax.axis_index("row"), lax.axis_index("col")
    xpos, core = row // CORES, row % CORES
    layers = ((wx1, wru1, wn1), (wx2, wru2, wn2))
    turns = (2, 1, chips - 1)

    def device(x, c, y):
        return {"row": CORES * x + c, "col": y}

    def wrap_x(v):
        return lax.rem(v + 2 * chips, chips)

    def wrap_y(v):
        return lax.rem(v + 2 * cols, cols)

    barrier = pltpu.get_barrier_semaphore()
    for k in range(1, rows * cols):
        other = {"row": lax.rem(row + k % rows, rows), "col": lax.rem(col + k // rows, cols)}
        pl.semaphore_signal(barrier, inc=1, device_id=other, device_id_type=MESH)
    pl.semaphore_wait(barrier, rows * cols - 1)

    def remote(src, dst, send, recv, to):
        return pltpu.make_async_remote_copy(
            src_ref=src, dst_ref=dst, send_sem=send, recv_sem=recv, device_id=to, device_id_type=MESH
        )

    def local(src, dst, sem):
        return pltpu.make_async_copy(src, dst, sem)

    def wait_for(ref, sem):
        pltpu.make_async_copy(ref, ref, sem).wait()

    def chunk_place(c, j, x_from, x_to, y_to):
        return chips * wrap_y(x_from - y_to) + wrap_x(HALVES * c + j - x_to)

    def recurrent_pieces(layer, j, x_to, dst):
        _, wru, wn = layers[layer]
        depth = pl.ds(j * chunk, chunk)
        for s in range(HALVES):
            units = pl.ds(pl.multiple_of(x_to * chunk + s * half, half), half)
            yield wru.at[:, depth, units], dst.at[pl.ds(0, 2), s]
            yield wn.at[depth, units], dst.at[2, s]

    def inputs_pieces(layer, j, x_to, dst):
        depth = pl.ds(j * chunk, chunk)
        for s in range(HALVES):
            units = pl.ds(pl.multiple_of(x_to * chunk + s * half, half), half)
            yield layers[layer][0].at[:, depth, units], dst.at[:, s]

    parts = (
        (recurrent_pieces, recurrent, recurrent_sem, recurrent_sent, 1),
        (inputs_pieces, inputs, inputs_sem, inputs_sent, 0),
    )

    def send_part(part, layer, turn):
        pieces, kept, sem, sent, to_core = part
        x_to = wrap_x(xpos + turn)
        for j in range(2):
            place = chunk_place(core, j, xpos, x_to, col)
            for src, dst in pieces(layer, j, x_to, kept.at[layer, place]):
                remote(src, dst, sent.at[layer, turn, j], sem.at[layer, place], device(x_to, to_core, col)).start()

    def keep_part(part, layer):
        pieces, kept, sem, _, c = part
        for j in range(2):
            place = chunk_place(c, j, xpos, xpos, col)
            for src, dst in pieces(layer, j, xpos, kept.at[layer, place]):
                local(src, dst, sem.at[layer, place]).start()

    def send_weights(layer):
        for turn in turns:
            for part in parts:
                send_part(part, layer, turn)

    def share_in_chip(layer):
        for part in parts:
            here = core == part[4]
            pl.when(here)(functools.partial(keep_part, part, layer))
            pl.when(jnp.logical_not(here))(functools.partial(send_part, part, layer, 0))

    def hand_over():
        for turn in turns:
            x_to = wrap_x(xpos + turn)
            for n, (pieces, _, _, sent, _) in enumerate(parts):
                for j in range(2):
                    for src, dst in pieces(1, j, x_to, recurrent.at[n, 2 * turn + j]):
                        remote(src, dst, sent.at[1, turn, j], hand_sem.at[n, turn, j], device(xpos, 0, col)).start()

    def send_handed():
        for turn in turns:
            x_to = wrap_x(xpos + turn)
            for n, (_, kept, sem, _, to_core) in enumerate(parts):
                for j in range(2):
                    src = recurrent.at[n, 2 * turn + j]
                    wait_for(src, hand_sem.at[n, turn, j])
                    place = chunk_place(1, j, xpos, x_to, col)
                    remote(src, kept.at[1, place], handed_sent.at[n, turn, j], sem.at[1, place], device(x_to, to_core, col)).start()

    share = steps // cols

    def share_of(y):
        return pl.ds(pl.multiple_of(y * share, share), share)

    my_share = share_of(col)

    def x_pieces(j, dst):
        for s in range(HALVES):
            yield x_ref.at[my_share, :, pl.ds(j * chunk + s * half, half)], dst.at[my_share, s]

    def send_x(turn):
        x_to = wrap_x(xpos + turn)
        for j in range(2):
            place = chunk_place(core, j, xpos, x_to, col)
            for src, dst in x_pieces(j, xs.at[place]):
                remote(src, dst, x_sent.at[turn, j], x_sem.at[place], device(x_to, 0, col)).start()

    def keep_x():
        for j in range(2):
            place = chunk_place(0, j, xpos, xpos, col)
            for src, dst in x_pieces(j, xs.at[place]):
                local(src, dst, x_sem.at[place]).start()

    def pass_x_on():
        for p in range(places):
            wait_for(xs.at[p, my_share], x_sem.at[p])
        for k in range(1, cols):
            for dy in range(cols):
                src = xs.at[pl.ds(chips * dy, chips), my_share]
                dst = xs.at[pl.ds(chips * ((dy - k) % cols), chips), my_share]
                remote(src, dst, x_passed.at[k], xs_sem.at[k], device(xpos, 0, wrap_y(col + k))).start()

    @pl.when(xpos == col)
    def _():
        for j in range(2):
            x_to = HALVES * core + j
            for s in range(HALVES):
                src = h_ref.at[:, :, pl.ds(j * chunk + s * half, half)]
                dst = state_in.at[:, s]
                mine = (x_to == xpos) & (core == 1)

                @pl.when(mine)
                def _():
                    local(src, dst, state_sem.at[s]).start()

                @pl.when(jnp.logical_not(mine))
                def _():
                    copy = remote(src, dst, state_sent.at[j, s], state_sem.at[s], device(x_to, 1, col))
                    copy.start()
                    copy.wait_send()

    for turn in turns:
        send_x(turn)
    pl.when(core == 1)(lambda: send_x(0))
    pl.when(core == 0)(keep_x)
    send_weights(0)
    share_in_chip(0)

    @pl.when(core == 1)
    def _():
        hand_over()

    @pl.when(core == 0)
    def _():
        pass_x_on()
        send_weights(1)

    share_in_chip(1)
    pl.when(core == 0)(send_handed)

    def drain_sends():
        piece = recurrent.at[0, 0]
        for layer in range(2):
            for j in range(2):
                for n, (_, _, _, sent, to_core) in enumerate(parts):
                    for turn in turns:
                        wait_for(piece, sent.at[layer, turn, j])

                    @pl.when(core != to_core)
                    def _():
                        wait_for(piece, sent.at[layer, 0, j])

        part = xs.at[0, my_share]
        for j in range(2):
            for turn in turns:
                wait_for(part, x_sent.at[turn, j])

        @pl.when(core == 0)
        def _():
            for n in range(len(parts)):
                for j in range(2):
                    for turn in turns:
                        wait_for(piece, handed_sent.at[n, turn, j])
            for k in range(1, cols):
                wait_for(xs.at[:, my_share], x_passed.at[k])

        @pl.when(core == 1)
        def _():
            for j in range(2):
                wait_for(part, x_sent.at[0, j])

    offsets = [(dx, dy) for dy in range(cols) for dx in range(chips)]
    distance = [ring_distance(dx, chips) + ring_distance(dy, cols) for dx, dy in offsets]
    far_first = sorted(range(1, places), key=lambda p: -distance[p])
    by_arrival = sorted(range(places), key=lambda p: (distance[p], ring_distance(offsets[p][0], chips)))

    def spread(blocks, kind):
        for p in far_first:
            dx, dy = offsets[p]
            there = chips * ((cols - dy) % cols) + (chips - dx) % chips
            to = device(wrap_x(xpos + dx), 1, wrap_y(col + dy))
            remote(blocks.at[0], blocks.at[there], block_sent.at[kind], block_sem.at[kind, there], to).start()

    def arrived(blocks, kind, p):
        wait_for(blocks.at[p], block_sem.at[kind, p])

    def all_sent(blocks, kind):
        wait_for(blocks.at[pl.ds(1, places - 1)], block_sent.at[kind])

    def wide(pieces):
        return jnp.concatenate(pieces, axis=1)

    def product(lhs_of, kept, layer, gates, order, before=None):
        total = None
        for p in order:
            if before is not None and p:
                before(p)
            rhs = wide([kept[layer, p, g, s] for g in gates for s in range(HALVES)])
            lhs = wide([lhs_of(p, s) for s in range(HALVES)])
            term = jnp.dot(lhs, rhs, preferred_element_type=F32)
            total = term if total is None else total + term
        return total

    def gathered(blocks, kind, layer, gate):
        return product(lambda p, s: blocks[p, s], recurrent, layer, (gate,), by_arrival, lambda p: arrived(blocks, kind, p))

    def halves_of(total, n=0):
        return [total[:, (n * HALVES + s) * half : (n * HALVES + s + 1) * half] for s in range(HALVES)]

    H1, R1, H2, R2 = range(4)

    def project(layer, lhs_of, bias, made):
        total = product(lhs_of, inputs, layer, (RESET, UPDATE, CAND), range(places))
        for g in range(3):
            for s, value in enumerate(halves_of(total, g)):
                here = bias[pl.ds(g, 1), pl.ds(pl.multiple_of(xpos * chunk + s * half, half), half)]
                made[g, s] = value + here

    def make_first(t, again):
        slot = lax.rem(t, 2)
        if again:
            wait_for(first_made.at[slot], first_sent.at[slot])
        project(0, lambda p, s: xs[p, t, s], b1, first_made.at[slot])
        remote(first_made.at[slot], first_p.at[slot], first_sent.at[slot], first_sem.at[slot], device(xpos, 1, col)).start()

    def make_second(again):
        if again:
            wait_for(second_made, second_sent)
        wait_for(h1_here, h1_sem)
        project(1, lambda p, s: h1_here[p, s], b2, second_made)
        remote(second_made, second_p, second_sent, second_sem, device(xpos, 1, col)).start()

    def reset_half(layer, blocks, kind, out_blocks, p_ref, before_send, after_send):
        total = gathered(blocks, kind, layer, RESET)
        before_send()
        for s, value in enumerate(halves_of(total)):
            reset = jax.nn.sigmoid(p_ref[RESET, s] + value)
            out_blocks[0, s] = (reset * states[layer, s]).astype(BF16)
        after_send()
        total = product(lambda p, s: blocks[p, s], recurrent, layer, (UPDATE,), range(places))
        for s, value in enumerate(halves_of(total)):
            updates[layer, s] = jax.nn.sigmoid(p_ref[UPDATE, s] + value)
        all_sent(blocks, kind)

    def next_half(layer, blocks, kind, p_ref, emit):
        total = gathered(blocks, kind, layer, CAND)
        for s, value in enumerate(halves_of(total)):
            candidate = jnp.tanh(p_ref[CAND, s] + value)
            update = updates[layer, s]
            state = (1.0 - update) * candidate + update * states[layer, s]
            emit(s, state.astype(BF16))
            states[layer, s] = state
        all_sent(blocks, kind)

    def hand_state(slot):
        remote(slot, h1_here, h1_sent, h1_sem, device(xpos, 0, col)).start()

    def first_reset(t, hand, handed):
        slot = h1_blocks.at[lax.rem(t, 2)]

        def before_send():
            wait_for(first_p.at[lax.rem(t, 2)], first_sem.at[lax.rem(t, 2)])
            if handed:
                wait_for(slot, h1_sent)

        def after_send():
            spread(r1_blocks, R1)
            if hand:
                hand_state(slot)

        reset_half(0, slot, H1, r1_blocks, first_p.at[lax.rem(t, 2)], before_send, after_send)

    def first_next(t):
        slot = h1_blocks.at[lax.rem(t + 1, 2)]

        def emit(s, value):
            slot[0, s] = value

        next_half(0, r1_blocks, R1, first_p.at[lax.rem(t, 2)], emit)
        spread(slot, H1)

    def second_reset(t):
        slot = h2_blocks.at[lax.rem(t, 2)]
        reset_half(
            1, slot, H2, r2_blocks, second_p, lambda: wait_for(second_p, second_sem), lambda: spread(r2_blocks, R2)
        )

    def second_next(t, last):
        slot = h2_blocks.at[lax.rem(t + 1, 2)]

        def emit(s, value):
            seq_halves[s, t] = value
            if not last:
                slot[0, s] = value

        next_half(1, r2_blocks, R2, second_p, emit)
        if not last:
            spread(slot, H2)

    def weights_here(kept, sem, layer):
        for p in range(places):
            wait_for(kept.at[layer, p], sem.at[layer, p])

    @pl.when(core == 1)
    def _():
        for s in range(HALVES):
            wait_for(state_in.at[:, s], state_sem.at[s])
        for layer in range(2):
            for s in range(HALVES):
                states[layer, s] = state_in[layer, s]
        for s in range(HALVES):
            h1_blocks[0, 0, s] = state_in[0, s].astype(BF16)
            h2_blocks[0, 0, s] = state_in[1, s].astype(BF16)
        spread(h1_blocks.at[0], H1)
        spread(h2_blocks.at[0], H2)
        weights_here(recurrent, recurrent_sem, 0)
        first_reset(0, False, False)
        first_next(0)
        weights_here(recurrent, recurrent_sem, 1)

        def step(t, handed):
            first_reset(t, True, handed)
            second_reset(t - 1)
            first_next(t)
            second_next(t - 1, False)

        def later_step(t, carry):
            step(t, True)
            return carry

        step(1, False)
        lax.fori_loop(2, steps, later_step, 0)
        last_slot = h1_blocks.at[steps % 2]
        for p in range(1, places):
            arrived(last_slot, H1, p)
        wait_for(last_slot, h1_sent)
        hand_state(last_slot)
        all_sent(last_slot, H1)
        second_reset(steps - 1)
        second_next(steps - 1, True)
        wait_for(last_slot, h1_sent)
        for layer in range(2):
            for s in range(HALVES):
                last_halves[s, layer] = states[layer, s]
        seq_copy = remote(seq_halves.at[0], seq_out, out_sent.at[0], out_sem.at[0], device(xpos, 0, col))
        last_copy = remote(last_halves.at[0], last_out, out_sent.at[1], out_sem.at[1], device(xpos, 0, col))
        seq_copy.start()
        last_copy.start()
        seq_out[...] = seq_halves[1]
        last_out[...] = last_halves[1]
        seq_copy.wait_send()
        last_copy.wait_send()

    @pl.when(core == 0)
    def _():
        for k in range(1, cols):
            wait_for(xs.at[:, share_of(wrap_y(col - k))], xs_sem.at[k])
        weights_here(inputs, inputs_sem, 0)
        make_first(0, False)
        make_first(1, False)
        weights_here(inputs, inputs_sem, 1)
        make_second(False)
        make_first(2, True)

        def later_step(t, carry):
            make_second(True)
            make_first(t + 1, True)
            return carry

        lax.fori_loop(2, steps - 1, later_step, 0)
        make_second(True)
        make_second(True)
        for slot in range(2):
            wait_for(first_made.at[slot], first_sent.at[slot])
        wait_for(second_made, second_sent)
        wait_for(seq_out, out_sem.at[0])
        wait_for(last_out, out_sem.at[1])

    drain_sends()


def solution(mesh):
    rows, cols = mesh.shape["row"], mesh.shape["col"]
    chips = rows // CORES
    places = chips * cols

    def device_body(x_rows, h_rows, wx_l1, whru_l1, whn_l1, bias_l1, wx_l2, whru_l2, whn_l2, bias_l2):
        steps, batch, row_block = x_rows.shape
        col_block = wx_l1.shape[2]
        half = col_block // rows
        chunk = HALVES * half
        anywhere = pl.BlockSpec(memory_space=pl.ANY)
        vmem = pl.BlockSpec(memory_space=pltpu.VMEM)
        dma = pltpu.SemaphoreType.DMA
        kinds = 4
        block = (HALVES, batch, half)
        scratch = [
            pltpu.VMEM((2, places, GATES, HALVES, chunk, half), BF16),
            pltpu.VMEM((2, places, GATES, HALVES, chunk, half), BF16),
            pltpu.VMEM((places, steps, *block), BF16),
            pltpu.VMEM((2, *block), F32),
            pltpu.VMEM((places, *block), BF16),
            pltpu.VMEM((2, places, *block), BF16),
            pltpu.VMEM((places, *block), BF16),
            pltpu.VMEM((2, places, *block), BF16),
            pltpu.VMEM((places, *block), BF16),
            pltpu.VMEM((2, GATES, *block), F32),
            pltpu.VMEM((GATES, *block), F32),
            pltpu.VMEM((2, GATES, *block), F32),
            pltpu.VMEM((GATES, *block), F32),
            pltpu.VMEM((2, *block), F32),
            pltpu.VMEM((2, *block), F32),
            pltpu.VMEM((HALVES, steps, batch, half), BF16),
            pltpu.VMEM((HALVES, 2, batch, half), F32),
            dma((2, places)),
            dma((2, places)),
            dma((2, chips, 2)),
            dma((places,)),
            dma((cols,)),
            dma((HALVES,)),
            dma((2, chips, 2)),
            dma((2, chips, 2)),
            dma((2, chips, 2)),
            dma((chips, 2)),
            dma((cols,)),
            dma((2, HALVES)),
            dma((kinds, places)),
            dma((kinds,)),
            dma,
            dma,
            dma((2,)),
            dma((2,)),
            dma,
            dma,
            dma((2,)),
            dma((2,)),
        ]
        return pl.pallas_call(
            functools.partial(gru_kernel, rows, cols),
            name="gru",
            out_shape=(
                jax.ShapeDtypeStruct((steps, batch, half), BF16),
                jax.ShapeDtypeStruct((2, batch, half), F32),
            ),
            in_specs=[anywhere, anywhere, anywhere, anywhere, anywhere, vmem, anywhere, anywhere, anywhere, vmem],
            out_specs=(vmem, vmem),
            scratch_shapes=scratch,
            compiler_params=pltpu.CompilerParams(
                collective_id=0, has_side_effects=True, vmem_limit_bytes=60 * 1024 * 1024
            ),
        )(
            x_rows, h_rows,
            jnp.transpose(wx_l1, (1, 0, 2)), jnp.transpose(whru_l1, (1, 0, 2)), whn_l1, bias_l1,
            jnp.transpose(wx_l2, (1, 0, 2)), jnp.transpose(whru_l2, (1, 0, 2)), whn_l2, bias_l2,
        )

    seq_spec = P(None, "data", "row")
    out_spec = P(None, "data", ("col", "row"))
    wide_spec = P("row", None, "col")
    square_spec = P("row", "col")
    bias_spec = P(None, "col")
    return jax.shard_map(
        device_body,
        mesh=mesh,
        in_specs=(seq_spec, seq_spec, wide_spec, wide_spec, square_spec, bias_spec, wide_spec, wide_spec, square_spec, bias_spec),
        out_specs=(out_spec, out_spec),
        check_vma=False,
    )
```

time: 435 us -> 443 us (1.018)
  Pallas kernels: 426 us -> 434 us
    pallas_call x1, Pallas kernels: 426 us -> 434 us  [device_body(): pl.pallas_call(functools.partial(gru_kernel, rows, cols), name='gru', out...]
where the time goes in v4:
time: 443 us
  Pallas kernels  434 us (98%)
  local copies, waits for them, and re-layouts  8.46 us (2%)
    pallas_call x1, Pallas kernels, device_body(): pl.pallas_call(functools.partial(gru_kernel, rows, cols), name='gru', out...  434 us

profile of v4, /device:TPU:97, one launch (start us, length us, event | category | flops | bytes accessed | tf_op | source)
XLA Modules:
  0.0 442.7 jit_solution(3340501387944487191)
XLA Ops:
  0.6 5.5 %copy_bitcast_fusion = (bf16[2,512,1024]{2,1,0:T(8,128)(2,1)}, bf16[2,512,1024]{2,1,0:T(8,128)(2,1)}) fusion(bf16[512,2,1024]{2,1,0:T(2,128)(2,1)} %param.17, bf16[512,2,1024]{2,1,0:T(2,128)(2,1)} %param.13), kind=kLoop, calls=%fused_computation | loop fusion | bytes 8388608 | tf_op jit(solution)/shard_map/transpose | solution.py:521
  6.1 433.6 %gru.1 = (bf16[24,32,128]{2,1,0:T(8,128)(2,1)}, f32[2,32,128]{2,1,0:T(8,128)}) custom-call(bf16[24,32,512]{2,1,0:T(8,128)(2,1)} %x_ref.1, f32[2,32,512]{2,1,0:T(8,128)} %h_ref.1, bf16[3,512,1024]{2,1,0:T(8,128)(2,1)} %bitcast.6, bf16[2,512,1024]{2,1,0:T(8,128)(2,1)} %get-tuple-element.3.wru1, bf16[512,1024]{1,0:T(8,128)(2,1)} %wn1.1, f32[3,1024]{1,0:T(4,128)} %b1.1, ...), custom_call_target="tpu_custom_call" | custom-call | tf_op jit(solution)/shard_map/gru/pallas_call | solution.py:505
  439.7 1.6 copy.18
  441.3 1.4 copy.19

commit v5 on v3

--- a/solution.py
+++ b/solution.py
@@ -207,7 +207,7 @@
     offsets = [(dx, dy) for dy in range(cols) for dx in range(chips)]
     distance = [ring_distance(dx, chips) + ring_distance(dy, cols) for dx, dy in offsets]
     far_first = sorted(range(1, places), key=lambda p: -distance[p])
-    by_arrival = sorted(range(places), key=lambda p: (distance[p], ring_distance(offsets[p][0], chips)))
+    by_arrival = [0] + far_first
 
     def spread(blocks, kind):
         for p in far_first:

time: 435 us -> 437 us (level)
  no operation moved by 1% of the time
where the time goes in v5:
time: 437 us
  Pallas kernels  428 us (98%)
  local copies, waits for them, and re-layouts  8.46 us (2%)
    pallas_call x1, Pallas kernels, device_body(): pl.pallas_call(functools.partial(gru_kernel, rows, cols), name='gru', out...  428 us

profile of v5, /device:TPU:97, one launch (start us, length us, event | category | flops | bytes accessed | tf_op | source)
XLA Modules:
  0.0 436.9 jit_solution(13932819801118544595)
XLA Ops:
  0.6 5.5 %copy_bitcast_fusion = (bf16[2,512,1024]{2,1,0:T(8,128)(2,1)}, bf16[2,512,1024]{2,1,0:T(8,128)(2,1)}) fusion(bf16[512,2,1024]{2,1,0:T(2,128)(2,1)} %param.17, bf16[512,2,1024]{2,1,0:T(2,128)(2,1)} %param.13), kind=kLoop, calls=%fused_computation | loop fusion | bytes 8388608 | tf_op jit(solution)/shard_map/transpose | solution.py:433
  6.1 427.8 %gru.1 = (bf16[24,32,128]{2,1,0:T(8,128)(2,1)}, f32[2,32,128]{2,1,0:T(8,128)}) custom-call(bf16[24,32,512]{2,1,0:T(8,128)(2,1)} %x_ref.1, f32[2,32,512]{2,1,0:T(8,128)} %h_ref.1, bf16[3,512,1024]{2,1,0:T(8,128)(2,1)} %bitcast.6, bf16[2,512,1024]{2,1,0:T(8,128)(2,1)} %get-tuple-element.3.wru1, bf16[512,1024]{1,0:T(8,128)(2,1)} %wn1.1, f32[3,1024]{1,0:T(4,128)} %b1.1, ...), custom_call_target="tpu_custom_call" | custom-call | tf_op jit(solution)/shard_map/gru/pallas_call | solution.py:417
  433.9 1.6 copy.18
  435.6 1.4 copy.19

commit v6 on v3

--- a/solution.py
+++ b/solution.py
@@ -14,6 +14,7 @@
 CORES = 2
 RESET, UPDATE, CAND, REC_RESET, REC_UPDATE, REC_CAND = range(6)
 GATES = 6
+EARLY = 2
 
 
 def ring_distance(offset, count):
@@ -24,11 +25,11 @@
     rows, cols,
     x_ref, h_ref, wx1, wru1, wn1, b1, wx2, wru2, wn2, b2,
     seq_out, last_out,
-    weights, xs, state_in,
+    weights, x_here, first_made, first_parts, state_in,
     h1_blocks, r1_blocks, h2_blocks, r2_blocks,
     states, updates, projections, seq_halves, last_halves,
-    weight_sem, hand_sem, x_sem, xs_sem, state_sem,
-    weight_sent, handed_sent, x_sent, x_passed, state_sent,
+    weight_sem, hand_sem, x_sem, wide_sem, parts_sem, state_sem,
+    weight_sent, handed_sent, x_sent, wide_sent, made_sent, state_sent,
     block_sem, block_sent, out_sem, out_sent,
 ):
     chips = rows // CORES
@@ -65,14 +66,27 @@
     def chunk_place(c, j, x_from, x_to, y_to):
         return place_of(HALVES * c + j, x_from, x_to, y_to)
 
-    def weight_pieces(layer, j, x_to, dst):
-        wx, wru, wn = layers[layer]
+    def input_pieces(layer, j, x_to, dst):
         depth = pl.ds(j * chunk, chunk)
         for s in range(HALVES):
             units = pl.ds(pl.multiple_of(x_to * chunk + s * half, half), half)
-            yield wx.at[:, depth, units], dst.at[pl.ds(0, 3), s]
+            yield layers[layer][0].at[:, depth, units], dst.at[pl.ds(0, 3), s]
+
+    def recurrent_pieces(layer, j, x_to, dst):
+        _, wru, wn = layers[layer]
+        depth = pl.ds(j * chunk, chunk)
+        for s in range(HALVES):
+            units = pl.ds(pl.multiple_of(x_to * chunk + s * half, half), half)
             yield wru.at[:, depth, units], dst.at[pl.ds(3, 2), s]
             yield wn.at[depth, units], dst.at[5, s]
+
+    def weight_pieces(layer, j, x_to, dst):
+        if layer:
+            yield from input_pieces(layer, j, x_to, dst)
+        yield from recurrent_pieces(layer, j, x_to, dst)
+
+    def moved(layer, index):
+        return weights.at[1, index] if layer else weights.at[0, index, pl.ds(3, 3)]
 
     def send_weights(layer, turns):
         for turn in turns:
@@ -104,36 +118,53 @@
                 place = chunk_place(1, j, xpos, x_to, col)
                 remote(src, weights.at[1, place], handed_sent.at[turn, j], weight_sem.at[1, place], device(x_to, 1, col)).start()
 
-    share = steps // cols
-    my_share = pl.ds(pl.multiple_of(col * share, share), share)
-
-    def x_pieces(j, dst):
-        for s in range(HALVES):
-            yield x_ref.at[my_share, :, pl.ds(j * chunk + s * half, half)], dst.at[my_share, s]
-
-    def send_x(turns):
-        for turn in turns:
-            x_to = wrap_x(xpos + turn)
-            for j in range(2):
-                place = chunk_place(core, j, xpos, x_to, col)
-                for src, dst in x_pieces(j, xs.at[place]):
-                    remote(src, dst, x_sent.at[turn, j], x_sem.at[place], device(x_to, 0, col)).start()
-
-    def keep_x():
+    def input_copies():
         for j in range(2):
-            place = chunk_place(0, j, xpos, xpos, col)
-            for src, dst in x_pieces(j, xs.at[place]):
-                pltpu.make_async_copy(src, dst, x_sem.at[place]).start()
-
-    def pass_x_on():
-        for p in range(places):
-            part = xs.at[p, my_share]
-            pltpu.make_async_copy(part, part, x_sem.at[p]).wait()
-        for k in range(cols):
-            for dy in range(cols):
-                src = xs.at[pl.ds(chips * dy, chips), my_share]
-                dst = xs.at[pl.ds(chips * ((dy - k) % cols), chips), my_share]
-                remote(src, dst, x_passed.at[k], xs_sem.at[col], device(xpos, 1, wrap_y(col + k))).start()
+            n = 2 * core + j
+            for s in range(HALVES):
+                yield x_ref.at[:, :, pl.ds(j * chunk + s * half, half)], x_here.at[n, :, s], x_sent.at[j], x_sem.at[n]
+            for turn in range(chips):
+                kept = weights.at[0, 2 * CORES * turn + n]
+                for src, dst in input_pieces(0, j, wrap_x(xpos + turn), kept):
+                    yield src, dst, wide_sent.at[turn, j], wide_sem.at[turn, n]
+
+    def keep_inputs():
+        for src, dst, _, sem in input_copies():
+            pltpu.make_async_copy(src, dst, sem).start()
+
+    def hand_inputs():
+        for src, dst, sent, sem in input_copies():
+            remote(src, dst, sent, sem, device(xpos, 0, col)).start()
+
+    def inputs_here():
+        for n in range(2 * CORES):
+            pltpu.make_async_copy(x_here.at[n], x_here.at[n], x_sem.at[n]).wait()
+            for turn in range(chips):
+                kept = weights.at[0, 2 * CORES * turn + n, pl.ds(0, 3)]
+                pltpu.make_async_copy(kept, kept, wide_sem.at[turn, n]).wait()
+
+    def wide(parts):
+        return jnp.concatenate(parts, axis=1)
+
+    def make_first(t, again):
+        slot = lax.rem(t, 2)
+        for turn in (2, 1, chips - 1, 0):
+            made = first_made.at[slot, turn]
+            if again:
+                pltpu.make_async_copy(made, made, made_sent.at[slot, turn]).wait()
+            total = None
+            for n in range(2 * CORES):
+                rhs = wide([weights[0, 2 * CORES * turn + n, g, s] for g in range(3) for s in range(HALVES)])
+                lhs = wide([x_here[n, t, s] for s in range(HALVES)])
+                term = jnp.dot(lhs, rhs, preferred_element_type=F32)
+                total = term if total is None else total + term
+            for g in range(3):
+                for s in range(HALVES):
+                    n = g * HALVES + s
+                    made[g, s] = total[:, n * half : (n + 1) * half]
+            seen = (chips - turn) % chips
+            to = device(wrap_x(xpos + turn), 1, col)
+            remote(made, first_parts.at[t, seen], made_sent.at[slot, turn], parts_sem.at[t, seen], to).start()
 
     far_turns = (2, 1, chips - 1)
 
@@ -156,28 +187,29 @@
                     copy.start()
                     copy.wait_send()
 
-    send_x(far_turns)
-    pl.when(core == 1)(lambda: send_x((0,)))
-    pl.when(core == 0)(keep_x)
     send_weights(0, far_turns)
 
     @pl.when(core == 1)
     def _():
+        hand_inputs()
         keep_weights(0)
         hand_over()
         keep_weights(1)
 
     @pl.when(core == 0)
     def _():
+        keep_inputs()
         send_weights(0, (0,))
-        pass_x_on()
+        inputs_here()
+        for t in range(EARLY):
+            make_first(t, False)
         send_weights(1, far_turns)
         send_weights(1, (0,))
         send_handed()
 
     def drain_sends():
-        piece = weights.at[0, 0]
         for layer in range(2):
+            piece = moved(layer, 0)
             for j in range(2):
                 for turn in far_turns:
                     pltpu.make_async_copy(piece, piece, weight_sent.at[layer, turn, j]).wait()
@@ -185,24 +217,25 @@
                 @pl.when(core == 0)
                 def _():
                     pltpu.make_async_copy(piece, piece, weight_sent.at[layer, 0, j]).wait()
-        part = xs.at[0, my_share]
-        for j in range(2):
-            for turn in far_turns:
-                pltpu.make_async_copy(part, part, x_sent.at[turn, j]).wait()
 
         @pl.when(core == 0)
         def _():
+            piece = moved(1, 0)
             for j in range(2):
                 for turn in far_turns:
                     pltpu.make_async_copy(piece, piece, handed_sent.at[turn, j]).wait()
-            whole = xs.at[:, my_share]
-            for k in range(cols):
-                pltpu.make_async_copy(whole, whole, x_passed.at[k]).wait()
+            for slot in range(2):
+                for turn in range(chips):
+                    made = first_made.at[slot, turn]
+                    pltpu.make_async_copy(made, made, made_sent.at[slot, turn]).wait()
 
         @pl.when(core == 1)
         def _():
-            for j in range(2):
-                pltpu.make_async_copy(part, part, x_sent.at[0, j]).wait()
+            piece = weights.at[0, 0, pl.ds(0, 3)]
+            for j in range(2):
+                pltpu.make_async_copy(x_here.at[0], x_here.at[0], x_sent.at[j]).wait()
+                for turn in range(chips):
+                    pltpu.make_async_copy(piece, piece, wide_sent.at[turn, j]).wait()
 
     offsets = [(dx, dy) for dy in range(cols) for dx in range(chips)]
     distance = [ring_distance(dx, chips) + ring_distance(dy, cols) for dx, dy in offsets]
@@ -222,9 +255,6 @@
     def all_sent(blocks, kind):
         sent = blocks.at[pl.ds(1, places - 1)]
         pltpu.make_async_copy(sent, sent, block_sent.at[kind]).wait()
-
-    def wide(parts):
-        return jnp.concatenate(parts, axis=1)
 
     def product(lhs_of, layer, gates, order, before=None):
         total = None
@@ -285,7 +315,13 @@
         spread(slot, H1)
 
     def first_inputs(t):
-        project(0, lambda p, s: xs[p, t, s], b1)
+        for n in range(chips):
+            part = first_parts.at[t, n]
+            pltpu.make_async_copy(part, part, parts_sem.at[t, n]).wait()
+        for g in range(3):
+            for s in range(HALVES):
+                here = b1[pl.ds(g, 1), pl.ds(pl.multiple_of(xpos * chunk + s * half, half), half)]
+                projections[0, g, s] = sum(first_parts[t, n, g, s] for n in range(chips)) + here
 
     def second_inputs(t):
         slot = h1_blocks.at[lax.rem(t, 2)]
@@ -322,15 +358,12 @@
             h2_blocks[0, 0, s] = state_in[1, s].astype(BF16)
         spread(h1_blocks.at[0], H1)
         spread(h2_blocks.at[0], H2)
-        for y in range(cols):
-            part = xs.at[:, pl.ds(y * share, share)]
-            pltpu.make_async_copy(part, part, xs_sem.at[y]).wait()
         for p in range(places):
-            pltpu.make_async_copy(weights.at[0, p], weights.at[0, p], weight_sem.at[0, p]).wait()
+            pltpu.make_async_copy(moved(0, p), moved(0, p), weight_sem.at[0, p]).wait()
         first_inputs(0)
         first_reset(0)
         first_next(0)
-        first_inputs(jnp.minimum(1, steps - 1))
+        first_inputs(1)
         for p in range(places):
             pltpu.make_async_copy(weights.at[1, p], weights.at[1, p], weight_sem.at[1, p]).wait()
 
@@ -340,7 +373,7 @@
             second_reset(t - 1)
             first_next(t)
             second_next(t - 1, False)
-            first_inputs(jnp.minimum(t + 1, steps - 1))
+            pl.when(t + 1 < steps)(lambda: first_inputs(t + 1))
             return carry
 
         lax.fori_loop(1, steps, step, 0)
@@ -365,6 +398,11 @@
 
     @pl.when(core == 0)
     def _():
+        def later_first(t, carry):
+            make_first(t, True)
+            return carry
+
+        lax.fori_loop(EARLY, steps, later_first, 0)
         pltpu.make_async_copy(seq_out, seq_out, out_sem.at[0]).wait()
         pltpu.make_async_copy(last_out, last_out, out_sem.at[1]).wait()
 
@@ -388,7 +426,9 @@
         block = (HALVES, batch, half)
         scratch = [
             pltpu.VMEM((2, places, GATES, HALVES, chunk, half), BF16),
-            pltpu.VMEM((places, steps, *block), BF16),
+            pltpu.VMEM((2 * CORES, steps, *block), BF16),
+            pltpu.VMEM((2, chips, 3, *block), F32),
+            pltpu.VMEM((steps, chips, 3, *block), F32),
             pltpu.VMEM((2, *block), F32),
             pltpu.VMEM((2, places, *block), BF16),
             pltpu.VMEM((places, *block), BF16),
@@ -401,13 +441,15 @@
             pltpu.VMEM((HALVES, 2, batch, half), F32),
             dma((2, places)),
             dma((chips, 2)),
-            dma((places,)),
-            dma((cols,)),
+            dma((2 * CORES,)),
+            dma((chips, 2 * CORES)),
+            dma((steps, chips)),
             dma((HALVES,)),
             dma((2, chips, 2)),
             dma((chips, 2)),
+            dma((2,)),
             dma((chips, 2)),
-            dma((cols,)),
+            dma((2, chips)),
             dma((2, HALVES)),
             dma((kinds, places)),
             dma((kinds,)),

time: 435 us -> 396 us (0.910)
  Pallas kernels: 426 us -> 387 us
    pallas_call x1, Pallas kernels: 426 us -> 387 us  [device_body(): pl.pallas_call(functools.partial(gru_kernel, rows, cols), name='gru', out...]
where the time goes in v6:
time: 396 us
  Pallas kernels  387 us (98%)
  local copies, waits for them, and re-layouts  8.46 us (2%)
    pallas_call x1, Pallas kernels, device_body(): pl.pallas_call(functools.partial(gru_kernel, rows, cols), name='gru', out...  387 us

profile of v6, /device:TPU:97, one launch (start us, length us, event | category | flops | bytes accessed | tf_op | source)
XLA Modules:
  0.0 395.8 jit_solution(8455540705134401793)
XLA Ops:
  0.6 5.5 %copy_bitcast_fusion = (bf16[2,512,1024]{2,1,0:T(8,128)(2,1)}, bf16[2,512,1024]{2,1,0:T(8,128)(2,1)}) fusion(bf16[512,2,1024]{2,1,0:T(2,128)(2,1)} %param.17, bf16[512,2,1024]{2,1,0:T(2,128)(2,1)} %param.13), kind=kLoop, calls=%fused_computation | loop fusion | bytes 8388608 | tf_op jit(solution)/shard_map/transpose | solution.py:475
  6.1 386.7 %gru.1 = (bf16[24,32,128]{2,1,0:T(8,128)(2,1)}, f32[2,32,128]{2,1,0:T(8,128)}) custom-call(bf16[24,32,512]{2,1,0:T(8,128)(2,1)} %x_ref.1, f32[2,32,512]{2,1,0:T(8,128)} %h_ref.1, bf16[3,512,1024]{2,1,0:T(8,128)(2,1)} %bitcast.6, bf16[2,512,1024]{2,1,0:T(8,128)(2,1)} %get-tuple-element.3.wru1, bf16[512,1024]{1,0:T(8,128)(2,1)} %wn1.1, f32[3,1024]{1,0:T(4,128)} %b1.1, ...), custom_call_target="tpu_custom_call" | custom-call | tf_op jit(solution)/shard_map/gru/pallas_call | solution.py:459
  392.8 1.6 copy.18
  394.4 1.4 copy.19

commit v7 on v6

--- a/solution.py
+++ b/solution.py
@@ -25,11 +25,11 @@
     rows, cols,
     x_ref, h_ref, wx1, wru1, wn1, b1, wx2, wru2, wn2, b2,
     seq_out, last_out,
-    weights, x_here, first_made, first_parts, state_in,
+    weights, x_here, h1_here, first_made, first_parts, second_made, second_parts, state_in,
     h1_blocks, r1_blocks, h2_blocks, r2_blocks,
     states, updates, projections, seq_halves, last_halves,
-    weight_sem, hand_sem, x_sem, wide_sem, parts_sem, state_sem,
-    weight_sent, handed_sent, x_sent, wide_sent, made_sent, state_sent,
+    weight_sem, hand_sem, x_sem, wide_sem, parts_sem, second_sem, h1_sem, state_sem,
+    weight_sent, handed_sent, x_sent, wide_sent, made_sent, second_sent, h1_sent, state_sent,
     block_sem, block_sent, out_sem, out_sent,
 ):
     chips = rows // CORES
@@ -80,91 +80,98 @@
             yield wru.at[:, depth, units], dst.at[pl.ds(3, 2), s]
             yield wn.at[depth, units], dst.at[5, s]
 
-    def weight_pieces(layer, j, x_to, dst):
-        if layer:
-            yield from input_pieces(layer, j, x_to, dst)
-        yield from recurrent_pieces(layer, j, x_to, dst)
-
     def moved(layer, index):
-        return weights.at[1, index] if layer else weights.at[0, index, pl.ds(3, 3)]
+        return weights.at[layer, index, pl.ds(3, 3)]
 
     def send_weights(layer, turns):
         for turn in turns:
             x_to = wrap_x(xpos + turn)
             for j in range(2):
                 place = chunk_place(core, j, xpos, x_to, col)
-                for src, dst in weight_pieces(layer, j, x_to, weights.at[layer, place]):
+                for src, dst in recurrent_pieces(layer, j, x_to, weights.at[layer, place]):
                     remote(src, dst, weight_sent.at[layer, turn, j], weight_sem.at[layer, place], device(x_to, 1, col)).start()
 
     def keep_weights(layer):
         for j in range(2):
             place = chunk_place(1, j, xpos, xpos, col)
-            for src, dst in weight_pieces(layer, j, xpos, weights.at[layer, place]):
+            for src, dst in recurrent_pieces(layer, j, xpos, weights.at[layer, place]):
                 pltpu.make_async_copy(src, dst, weight_sem.at[layer, place]).start()
 
     def hand_over():
         for turn in far_turns:
             x_to = wrap_x(xpos + turn)
             for j in range(2):
-                for src, dst in weight_pieces(1, j, x_to, weights.at[1, 2 * turn + j]):
+                for src, dst in recurrent_pieces(1, j, x_to, weights.at[1, 2 * turn + j]):
                     remote(src, dst, weight_sent.at[1, turn, j], hand_sem.at[turn, j], device(xpos, 0, col)).start()
 
     def send_handed():
         for turn in far_turns:
             x_to = wrap_x(xpos + turn)
             for j in range(2):
-                src = weights.at[1, 2 * turn + j]
+                src = moved(1, 2 * turn + j)
                 pltpu.make_async_copy(src, src, hand_sem.at[turn, j]).wait()
                 place = chunk_place(1, j, xpos, x_to, col)
-                remote(src, weights.at[1, place], handed_sent.at[turn, j], weight_sem.at[1, place], device(x_to, 1, col)).start()
-
-    def input_copies():
+                remote(src, moved(1, place), handed_sent.at[turn, j], weight_sem.at[1, place], device(x_to, 1, col)).start()
+
+    def x_copies():
         for j in range(2):
             n = 2 * core + j
             for s in range(HALVES):
                 yield x_ref.at[:, :, pl.ds(j * chunk + s * half, half)], x_here.at[n, :, s], x_sent.at[j], x_sem.at[n]
-            for turn in range(chips):
-                kept = weights.at[0, 2 * CORES * turn + n]
-                for src, dst in input_pieces(0, j, wrap_x(xpos + turn), kept):
-                    yield src, dst, wide_sent.at[turn, j], wide_sem.at[turn, n]
-
-    def keep_inputs():
-        for src, dst, _, sem in input_copies():
+
+    def input_copies(layer):
+        for turn in range(chips):
+            for j in range(2):
+                n = 2 * core + j
+                for src, dst in input_pieces(layer, j, wrap_x(xpos + turn), weights.at[layer, 2 * CORES * turn + n]):
+                    yield src, dst, wide_sent.at[layer, turn, j], wide_sem.at[layer, turn, n]
+
+    def keep(copies):
+        for src, dst, _, sem in copies:
             pltpu.make_async_copy(src, dst, sem).start()
 
-    def hand_inputs():
-        for src, dst, sent, sem in input_copies():
+    def hand(copies):
+        for src, dst, sent, sem in copies:
             remote(src, dst, sent, sem, device(xpos, 0, col)).start()
 
-    def inputs_here():
+    def x_arrived():
         for n in range(2 * CORES):
             pltpu.make_async_copy(x_here.at[n], x_here.at[n], x_sem.at[n]).wait()
-            for turn in range(chips):
-                kept = weights.at[0, 2 * CORES * turn + n, pl.ds(0, 3)]
-                pltpu.make_async_copy(kept, kept, wide_sem.at[turn, n]).wait()
+
+    def inputs_arrived(layer):
+        for turn in range(chips):
+            for n in range(2 * CORES):
+                kept = weights.at[layer, 2 * CORES * turn + n, pl.ds(0, 3)]
+                pltpu.make_async_copy(kept, kept, wide_sem.at[layer, turn, n]).wait()
 
     def wide(parts):
         return jnp.concatenate(parts, axis=1)
 
-    def make_first(t, again):
-        slot = lax.rem(t, 2)
+    def make(layer, lhs_of, made, sent, parts, sem, again):
         for turn in (2, 1, chips - 1, 0):
-            made = first_made.at[slot, turn]
             if again:
-                pltpu.make_async_copy(made, made, made_sent.at[slot, turn]).wait()
+                pltpu.make_async_copy(made.at[turn], made.at[turn], sent.at[turn]).wait()
             total = None
             for n in range(2 * CORES):
-                rhs = wide([weights[0, 2 * CORES * turn + n, g, s] for g in range(3) for s in range(HALVES)])
-                lhs = wide([x_here[n, t, s] for s in range(HALVES)])
+                rhs = wide([weights[layer, 2 * CORES * turn + n, g, s] for g in range(3) for s in range(HALVES)])
+                lhs = wide([lhs_of(n, s) for s in range(HALVES)])
                 term = jnp.dot(lhs, rhs, preferred_element_type=F32)
                 total = term if total is None else total + term
             for g in range(3):
                 for s in range(HALVES):
                     n = g * HALVES + s
-                    made[g, s] = total[:, n * half : (n + 1) * half]
+                    made[turn, g, s] = total[:, n * half : (n + 1) * half]
             seen = (chips - turn) % chips
-            to = device(wrap_x(xpos + turn), 1, col)
-            remote(made, first_parts.at[t, seen], made_sent.at[slot, turn], parts_sem.at[t, seen], to).start()
+            remote(made.at[turn], parts.at[seen], sent.at[turn], sem.at[seen], device(wrap_x(xpos + turn), 1, col)).start()
+
+    def make_first(t, again):
+        slot = lax.rem(t, 2)
+        make(0, lambda n, s: x_here[n, t, s], first_made.at[slot], made_sent.at[slot], first_parts.at[t], parts_sem.at[t], again)
+
+    def make_second(t, again):
+        slot = lax.rem(t, 2)
+        pltpu.make_async_copy(h1_here, h1_here, h1_sem).wait()
+        make(1, lambda n, s: h1_here[wrap_x(n - xpos), s], second_made, second_sent, second_parts.at[slot], second_sem.at[slot], again)
 
     far_turns = (2, 1, chips - 1)
 
@@ -191,25 +198,30 @@
 
     @pl.when(core == 1)
     def _():
-        hand_inputs()
+        hand(x_copies())
+        hand(input_copies(0))
         keep_weights(0)
         hand_over()
+        hand(input_copies(1))
         keep_weights(1)
 
     @pl.when(core == 0)
     def _():
-        keep_inputs()
+        keep(x_copies())
+        keep(input_copies(0))
         send_weights(0, (0,))
-        inputs_here()
+        x_arrived()
+        inputs_arrived(0)
         for t in range(EARLY):
             make_first(t, False)
         send_weights(1, far_turns)
         send_weights(1, (0,))
+        keep(input_copies(1))
         send_handed()
 
     def drain_sends():
+        piece = moved(0, 0)
         for layer in range(2):
-            piece = moved(layer, 0)
             for j in range(2):
                 for turn in far_turns:
                     pltpu.make_async_copy(piece, piece, weight_sent.at[layer, turn, j]).wait()
@@ -220,22 +232,22 @@
 
         @pl.when(core == 0)
         def _():
-            piece = moved(1, 0)
             for j in range(2):
                 for turn in far_turns:
                     pltpu.make_async_copy(piece, piece, handed_sent.at[turn, j]).wait()
-            for slot in range(2):
-                for turn in range(chips):
-                    made = first_made.at[slot, turn]
+            for turn in range(chips):
+                made = second_made.at[turn]
+                pltpu.make_async_copy(made, made, second_sent.at[turn]).wait()
+                for slot in range(2):
                     pltpu.make_async_copy(made, made, made_sent.at[slot, turn]).wait()
 
         @pl.when(core == 1)
         def _():
-            piece = weights.at[0, 0, pl.ds(0, 3)]
             for j in range(2):
                 pltpu.make_async_copy(x_here.at[0], x_here.at[0], x_sent.at[j]).wait()
-                for turn in range(chips):
-                    pltpu.make_async_copy(piece, piece, wide_sent.at[turn, j]).wait()
+                for layer in range(2):
+                    for turn in range(chips):
+                        pltpu.make_async_copy(piece, piece, wide_sent.at[layer, turn, j]).wait()
 
     offsets = [(dx, dy) for dy in range(cols) for dx in range(chips)]
     distance = [ring_distance(dx, chips) + ring_distance(dy, cols) for dx, dy in offsets]
@@ -270,13 +282,13 @@
     def gathered(blocks, kind, layer, gate):
         return product(lambda p, s: blocks[p, s], layer, (gate,), by_arrival, lambda p: arrived(blocks, kind, p))
 
-    def project(layer, lhs_of, bias):
-        total = product(lhs_of, layer, (RESET, UPDATE, CAND), range(places))
+    def add_parts(layer, parts, sem, bias):
+        for n in range(chips):
+            pltpu.make_async_copy(parts.at[n], parts.at[n], sem.at[n]).wait()
         for g in range(3):
             for s in range(HALVES):
-                n = g * HALVES + s
                 here = bias[pl.ds(g, 1), pl.ds(pl.multiple_of(xpos * chunk + s * half, half), half)]
-                projections[layer, g, s] = total[:, n * half : (n + 1) * half] + here
+                projections[layer, g, s] = sum(parts[n, g, s] for n in range(chips)) + here
 
     def reset_half(layer, blocks, kind, out_blocks, send):
         total = gathered(blocks, kind, layer, REC_RESET)
@@ -299,9 +311,19 @@
 
     H1, R1, H2, R2 = range(4)
 
-    def first_reset(t):
+    def hand_state(slot):
+        four = slot.at[pl.ds(chips * wrap_y(xpos - col), chips)]
+        return remote(four, h1_here, h1_sent, h1_sem, device(xpos, 0, col))
+
+    def first_reset(t, handed):
         slot = h1_blocks.at[lax.rem(t, 2)]
-        reset_half(0, slot, H1, r1_blocks, lambda: spread(r1_blocks, R1))
+
+        def send():
+            spread(r1_blocks, R1)
+            if handed:
+                hand_state(slot).start()
+
+        reset_half(0, slot, H1, r1_blocks, send)
         all_sent(slot, H1)
 
     def first_next(t):
@@ -315,17 +337,12 @@
         spread(slot, H1)
 
     def first_inputs(t):
-        for n in range(chips):
-            part = first_parts.at[t, n]
-            pltpu.make_async_copy(part, part, parts_sem.at[t, n]).wait()
-        for g in range(3):
-            for s in range(HALVES):
-                here = b1[pl.ds(g, 1), pl.ds(pl.multiple_of(xpos * chunk + s * half, half), half)]
-                projections[0, g, s] = sum(first_parts[t, n, g, s] for n in range(chips)) + here
+        add_parts(0, first_parts.at[t], parts_sem.at[t], b1)
 
     def second_inputs(t):
-        slot = h1_blocks.at[lax.rem(t, 2)]
-        project(1, lambda p, s: slot[p, s], b2)
+        hand_state(h1_blocks.at[lax.rem(t + 1, 2)]).wait_send()
+        slot = lax.rem(t, 2)
+        add_parts(1, second_parts.at[slot], second_sem.at[slot], b2)
 
     def second_reset(t):
         slot = h2_blocks.at[lax.rem(t, 2)]
@@ -361,27 +378,34 @@
         for p in range(places):
             pltpu.make_async_copy(moved(0, p), moved(0, p), weight_sem.at[0, p]).wait()
         first_inputs(0)
-        first_reset(0)
+        first_reset(0, False)
         first_next(0)
         first_inputs(1)
+        first_reset(1, True)
+        first_next(1)
         for p in range(places):
-            pltpu.make_async_copy(weights.at[1, p], weights.at[1, p], weight_sem.at[1, p]).wait()
+            pltpu.make_async_copy(moved(1, p), moved(1, p), weight_sem.at[1, p]).wait()
+        second_inputs(0)
+        second_reset(0)
+        first_inputs(2)
 
         def step(t, carry):
-            first_reset(t)
-            second_inputs(t)
+            first_reset(t, True)
+            second_next(t - 2, False)
+            first_next(t)
+            second_inputs(t - 1)
             second_reset(t - 1)
-            first_next(t)
-            second_next(t - 1, False)
             pl.when(t + 1 < steps)(lambda: first_inputs(t + 1))
             return carry
 
-        lax.fori_loop(1, steps, step, 0)
+        lax.fori_loop(2, steps, step, 0)
         last_slot = h1_blocks.at[steps % 2]
         for p in range(1, places):
             arrived(last_slot, H1, p)
+        hand_state(last_slot).start()
         all_sent(last_slot, H1)
-        second_inputs(steps)
+        second_next(steps - 2, False)
+        second_inputs(steps - 1)
         second_reset(steps - 1)
         second_next(steps - 1, True)
         for layer in range(2):
@@ -398,11 +422,17 @@
 
     @pl.when(core == 0)
     def _():
-        def later_first(t, carry):
-            make_first(t, True)
+        inputs_arrived(1)
+        make_first(EARLY, True)
+        make_second(0, False)
+        make_first(EARLY + 1, True)
+
+        def later(t, carry):
+            make_second(t, True)
+            pl.when(t + EARLY + 1 < steps)(lambda: make_first(t + EARLY + 1, True))
             return carry
 
-        lax.fori_loop(EARLY, steps, later_first, 0)
+        lax.fori_loop(1, steps, later, 0)
         pltpu.make_async_copy(seq_out, seq_out, out_sem.at[0]).wait()
         pltpu.make_async_copy(last_out, last_out, out_sem.at[1]).wait()
 
@@ -427,8 +457,11 @@
         scratch = [
             pltpu.VMEM((2, places, GATES, HALVES, chunk, half), BF16),
             pltpu.VMEM((2 * CORES, steps, *block), BF16),
+            pltpu.VMEM((chips, *block), BF16),
             pltpu.VMEM((2, chips, 3, *block), F32),
             pltpu.VMEM((steps, chips, 3, *block), F32),
+            pltpu.VMEM((chips, 3, *block), F32),
+            pltpu.VMEM((2, chips, 3, *block), F32),
             pltpu.VMEM((2, *block), F32),
             pltpu.VMEM((2, places, *block), BF16),
             pltpu.VMEM((places, *block), BF16),
@@ -442,14 +475,18 @@
             dma((2, places)),
             dma((chips, 2)),
             dma((2 * CORES,)),
-            dma((chips, 2 * CORES)),
+            dma((2, chips, 2 * CORES)),
             dma((steps, chips)),
+            dma((2, chips)),
+            dma,
             dma((HALVES,)),
             dma((2, chips, 2)),
             dma((chips, 2)),
             dma((2,)),
-            dma((chips, 2)),
+            dma((2, chips, 2)),
             dma((2, chips)),
+            dma((chips,)),
+            dma,
             dma((2, HALVES)),
             dma((kinds, places)),
             dma((kinds,)),

time: 396 us -> 398 us (level)
  no operation moved by 1% of the time
where the time goes in v7:
time: 398 us
  Pallas kernels  389 us (98%)
  local copies, waits for them, and re-layouts  8.46 us (2%)
    pallas_call x1, Pallas kernels, device_body(): pl.pallas_call(functools.partial(gru_kernel, rows, cols), name='gru', out...  389 us

profile of v7, /device:TPU:97, one launch (start us, length us, event | category | flops | bytes accessed | tf_op | source)
XLA Modules:
  0.0 398.1 jit_solution(1320876471094652427)
XLA Ops:
  0.6 5.5 %copy_bitcast_fusion = (bf16[2,512,1024]{2,1,0:T(8,128)(2,1)}, bf16[2,512,1024]{2,1,0:T(8,128)(2,1)}) fusion(bf16[512,2,1024]{2,1,0:T(2,128)(2,1)} %param.17, bf16[512,2,1024]{2,1,0:T(2,128)(2,1)} %param.13), kind=kLoop, calls=%fused_computation | loop fusion | bytes 8388608 | tf_op jit(solution)/shard_map/transpose | solution.py:512
  6.1 389.0 %gru.1 = (bf16[24,32,128]{2,1,0:T(8,128)(2,1)}, f32[2,32,128]{2,1,0:T(8,128)}) custom-call(bf16[24,32,512]{2,1,0:T(8,128)(2,1)} %x_ref.1, f32[2,32,512]{2,1,0:T(8,128)} %h_ref.1, bf16[3,512,1024]{2,1,0:T(8,128)(2,1)} %bitcast.6, bf16[2,512,1024]{2,1,0:T(8,128)(2,1)} %get-tuple-element.3.wru1, bf16[512,1024]{1,0:T(8,128)(2,1)} %wn1.1, f32[3,1024]{1,0:T(4,128)} %b1.1, ...), custom_call_target="tpu_custom_call" | custom-call | tf_op jit(solution)/shard_map/gru/pallas_call | solution.py:496
  395.1 1.6 copy.18
  396.7 1.4 copy.19

commit v8 on v6

--- a/solution.py
+++ b/solution.py
@@ -12,8 +12,9 @@
 BF16 = jnp.bfloat16
 HALVES = 2
 CORES = 2
-RESET, UPDATE, CAND, REC_RESET, REC_UPDATE, REC_CAND = range(6)
+RESET, UPDATE, CAND, REC_CAND, REC_RESET, REC_UPDATE = range(6)
 GATES = 6
+PAIR, WX, WN = range(3)
 EARLY = 2
 
 
@@ -25,7 +26,7 @@
     rows, cols,
     x_ref, h_ref, wx1, wru1, wn1, b1, wx2, wru2, wn2, b2,
     seq_out, last_out,
-    weights, x_here, first_made, first_parts, state_in,
+    weights, pairs, x_here, first_made, first_parts, state_in,
     h1_blocks, r1_blocks, h2_blocks, r2_blocks,
     states, updates, projections, seq_halves, last_halves,
     weight_sem, hand_sem, x_sem, wide_sem, parts_sem, state_sem,
@@ -66,57 +67,77 @@
     def chunk_place(c, j, x_from, x_to, y_to):
         return place_of(HALVES * c + j, x_from, x_to, y_to)
 
-    def input_pieces(layer, j, x_to, dst):
+    def room(part, layer, index):
+        if part == PAIR:
+            return pairs.at[layer, index]
+        return weights.at[layer, index, pl.ds(0, 3)] if part == WX else weights.at[layer, index, REC_CAND]
+
+    def pieces(part, layer, j, x_to, index):
         depth = pl.ds(j * chunk, chunk)
+        dst = room(part, layer, index)
+        wx, wru, wn = layers[layer]
         for s in range(HALVES):
             units = pl.ds(pl.multiple_of(x_to * chunk + s * half, half), half)
-            yield layers[layer][0].at[:, depth, units], dst.at[pl.ds(0, 3), s]
-
-    def recurrent_pieces(layer, j, x_to, dst):
-        _, wru, wn = layers[layer]
-        depth = pl.ds(j * chunk, chunk)
-        for s in range(HALVES):
-            units = pl.ds(pl.multiple_of(x_to * chunk + s * half, half), half)
-            yield wru.at[:, depth, units], dst.at[pl.ds(3, 2), s]
-            yield wn.at[depth, units], dst.at[5, s]
-
-    def weight_pieces(layer, j, x_to, dst):
-        if layer:
-            yield from input_pieces(layer, j, x_to, dst)
-        yield from recurrent_pieces(layer, j, x_to, dst)
-
-    def moved(layer, index):
-        return weights.at[1, index] if layer else weights.at[0, index, pl.ds(3, 3)]
-
-    def send_weights(layer, turns):
+            if part == PAIR:
+                yield wru.at[depth, :, units], dst.at[s]
+            elif part == WX:
+                yield wx.at[:, depth, units], dst.at[:, s]
+            else:
+                yield wn.at[depth, units], dst.at[s]
+
+    moving = ((PAIR, WN), (PAIR, WX, WN))
+
+    def send_part(part, layer, turns):
         for turn in turns:
             x_to = wrap_x(xpos + turn)
             for j in range(2):
                 place = chunk_place(core, j, xpos, x_to, col)
-                for src, dst in weight_pieces(layer, j, x_to, weights.at[layer, place]):
-                    remote(src, dst, weight_sent.at[layer, turn, j], weight_sem.at[layer, place], device(x_to, 1, col)).start()
+                sent, sem = weight_sent.at[layer, part, turn, j], weight_sem.at[layer, part, place]
+                for src, dst in pieces(part, layer, j, x_to, place):
+                    remote(src, dst, sent, sem, device(x_to, 1, col)).start()
 
     def keep_weights(layer):
-        for j in range(2):
-            place = chunk_place(1, j, xpos, xpos, col)
-            for src, dst in weight_pieces(layer, j, xpos, weights.at[layer, place]):
-                pltpu.make_async_copy(src, dst, weight_sem.at[layer, place]).start()
+        for part in moving[layer]:
+            for j in range(2):
+                place = chunk_place(1, j, xpos, xpos, col)
+                for src, dst in pieces(part, layer, j, xpos, place):
+                    pltpu.make_async_copy(src, dst, weight_sem.at[layer, part, place]).start()
 
     def hand_over():
+        for part in moving[1]:
+            for turn in far_turns:
+                x_to = wrap_x(xpos + turn)
+                for j in range(2):
+                    for src, dst in pieces(part, 1, j, x_to, 2 * turn + j):
+                        to = device(xpos, 0, col)
+                        remote(src, dst, weight_sent.at[1, part, turn, j], hand_sem.at[part, turn, j], to).start()
+
+    def send_handed(part):
         for turn in far_turns:
             x_to = wrap_x(xpos + turn)
             for j in range(2):
-                for src, dst in weight_pieces(1, j, x_to, weights.at[1, 2 * turn + j]):
-                    remote(src, dst, weight_sent.at[1, turn, j], hand_sem.at[turn, j], device(xpos, 0, col)).start()
-
-    def send_handed():
-        for turn in far_turns:
-            x_to = wrap_x(xpos + turn)
-            for j in range(2):
-                src = weights.at[1, 2 * turn + j]
-                pltpu.make_async_copy(src, src, hand_sem.at[turn, j]).wait()
+                src = room(part, 1, 2 * turn + j)
+                pltpu.make_async_copy(src, src, hand_sem.at[part, turn, j]).wait()
                 place = chunk_place(1, j, xpos, x_to, col)
-                remote(src, weights.at[1, place], handed_sent.at[turn, j], weight_sem.at[1, place], device(x_to, 1, col)).start()
+                sent, sem = handed_sent.at[part, turn, j], weight_sem.at[1, part, place]
+                remote(src, room(part, 1, place), sent, sem, device(x_to, 1, col)).start()
+
+    def weights_arrived(part, layer):
+        for p in range(places):
+            here = room(part, layer, p)
+            pltpu.make_async_copy(here, here, weight_sem.at[layer, part, p]).wait()
+
+    def split_pairs(layer):
+        def split(p, carry):
+            here = pairs.at[layer, p]
+            pltpu.make_async_copy(here, here, weight_sem.at[layer, PAIR, p]).wait()
+            for s in range(HALVES):
+                both = jnp.swapaxes(here[s], 0, 1)
+                weights[layer, p, REC_RESET, s] = both[0]
+                weights[layer, p, REC_UPDATE, s] = both[1]
+            return carry
+
+        lax.fori_loop(0, places, split, 0)
 
     def input_copies():
         for j in range(2):
@@ -124,8 +145,7 @@
             for s in range(HALVES):
                 yield x_ref.at[:, :, pl.ds(j * chunk + s * half, half)], x_here.at[n, :, s], x_sent.at[j], x_sem.at[n]
             for turn in range(chips):
-                kept = weights.at[0, 2 * CORES * turn + n]
-                for src, dst in input_pieces(0, j, wrap_x(xpos + turn), kept):
+                for src, dst in pieces(WX, 0, j, wrap_x(xpos + turn), 2 * CORES * turn + n):
                     yield src, dst, wide_sent.at[turn, j], wide_sem.at[turn, n]
 
     def keep_inputs():
@@ -187,7 +207,8 @@
                     copy.start()
                     copy.wait_send()
 
-    send_weights(0, far_turns)
+    for part in moving[0]:
+        send_part(part, 0, far_turns)
 
     @pl.when(core == 1)
     def _():
@@ -199,31 +220,36 @@
     @pl.when(core == 0)
     def _():
         keep_inputs()
-        send_weights(0, (0,))
+        for part in moving[0]:
+            send_part(part, 0, (0,))
         inputs_here()
         for t in range(EARLY):
             make_first(t, False)
-        send_weights(1, far_turns)
-        send_weights(1, (0,))
-        send_handed()
+        for part in moving[1]:
+            send_part(part, 1, far_turns)
+            send_part(part, 1, (0,))
+            send_handed(part)
 
     def drain_sends():
         for layer in range(2):
-            piece = moved(layer, 0)
-            for j in range(2):
-                for turn in far_turns:
-                    pltpu.make_async_copy(piece, piece, weight_sent.at[layer, turn, j]).wait()
-
-                @pl.when(core == 0)
-                def _():
-                    pltpu.make_async_copy(piece, piece, weight_sent.at[layer, 0, j]).wait()
+            for part in moving[layer]:
+                piece = room(part, layer, 0)
+                for j in range(2):
+                    for turn in far_turns:
+                        pltpu.make_async_copy(piece, piece, weight_sent.at[layer, part, turn, j]).wait()
 
         @pl.when(core == 0)
         def _():
-            piece = moved(1, 0)
-            for j in range(2):
-                for turn in far_turns:
-                    pltpu.make_async_copy(piece, piece, handed_sent.at[turn, j]).wait()
+            for layer in range(2):
+                for part in moving[layer]:
+                    piece = room(part, layer, 0)
+                    for j in range(2):
+                        pltpu.make_async_copy(piece, piece, weight_sent.at[layer, part, 0, j]).wait()
+            for part in moving[1]:
+                piece = room(part, 1, 0)
+                for j in range(2):
+                    for turn in far_turns:
+                        pltpu.make_async_copy(piece, piece, handed_sent.at[part, turn, j]).wait()
             for slot in range(2):
                 for turn in range(chips):
                     made = first_made.at[slot, turn]
@@ -231,7 +257,7 @@
 
         @pl.when(core == 1)
         def _():
-            piece = weights.at[0, 0, pl.ds(0, 3)]
+            piece = room(WX, 0, 0)
             for j in range(2):
                 pltpu.make_async_copy(x_here.at[0], x_here.at[0], x_sent.at[j]).wait()
                 for turn in range(chips):
@@ -241,6 +267,7 @@
     distance = [ring_distance(dx, chips) + ring_distance(dy, cols) for dx, dy in offsets]
     far_first = sorted(range(1, places), key=lambda p: -distance[p])
     by_arrival = sorted(range(places), key=lambda p: (distance[p], ring_distance(offsets[p][0], chips)))
+    groups = [by_arrival[:6], by_arrival[6:10], by_arrival[10:]]
 
     def spread(blocks, kind):
         for p in far_first:
@@ -256,11 +283,8 @@
         sent = blocks.at[pl.ds(1, places - 1)]
         pltpu.make_async_copy(sent, sent, block_sent.at[kind]).wait()
 
-    def product(lhs_of, layer, gates, order, before=None):
-        total = None
+    def product(lhs_of, layer, gates, order, total=None):
         for p in order:
-            if before is not None and p:
-                before(p)
             rhs = wide([weights[layer, p, g, s] for g in gates for s in range(HALVES)])
             lhs = wide([lhs_of(p, s) for s in range(HALVES)])
             term = jnp.dot(lhs, rhs, preferred_element_type=F32)
@@ -268,7 +292,13 @@
         return total
 
     def gathered(blocks, kind, layer, gate):
-        return product(lambda p, s: blocks[p, s], layer, (gate,), by_arrival, lambda p: arrived(blocks, kind, p))
+        total = None
+        for group in groups:
+            for p in group:
+                if p:
+                    arrived(blocks, kind, p)
+            total = product(lambda p, s: blocks[p, s], layer, (gate,), group, total)
+        return total
 
     def project(layer, lhs_of, bias):
         total = product(lhs_of, layer, (RESET, UPDATE, CAND), range(places))
@@ -311,8 +341,8 @@
             slot[0, s] = value
 
         next_half(0, r1_blocks, R1, emit)
+        spread(slot, H1)
         all_sent(r1_blocks, R1)
-        spread(slot, H1)
 
     def first_inputs(t):
         for n in range(chips):
@@ -341,9 +371,9 @@
                 slot[0, s] = value
 
         next_half(1, r2_blocks, R2, emit)
-        all_sent(r2_blocks, R2)
         if not last:
             spread(slot, H2)
+        all_sent(r2_blocks, R2)
 
     @pl.when(core == 1)
     def _():
@@ -358,25 +388,31 @@
             h2_blocks[0, 0, s] = state_in[1, s].astype(BF16)
         spread(h1_blocks.at[0], H1)
         spread(h2_blocks.at[0], H2)
-        for p in range(places):
-            pltpu.make_async_copy(moved(0, p), moved(0, p), weight_sem.at[0, p]).wait()
+        split_pairs(0)
+        weights_arrived(WN, 0)
         first_inputs(0)
         first_reset(0)
         first_next(0)
         first_inputs(1)
-        for p in range(places):
-            pltpu.make_async_copy(weights.at[1, p], weights.at[1, p], weight_sem.at[1, p]).wait()
-
-        def step(t, carry):
+        split_pairs(1)
+        weights_arrived(WX, 1)
+
+        def step(t, first):
             first_reset(t)
             second_inputs(t)
             second_reset(t - 1)
             first_next(t)
+            if first:
+                weights_arrived(WN, 1)
             second_next(t - 1, False)
             pl.when(t + 1 < steps)(lambda: first_inputs(t + 1))
+
+        def later_step(t, carry):
+            step(t, False)
             return carry
 
-        lax.fori_loop(1, steps, step, 0)
+        step(1, True)
+        lax.fori_loop(2, steps, later_step, 0)
         last_slot = h1_blocks.at[steps % 2]
         for p in range(1, places):
             arrived(last_slot, H1, p)
@@ -426,6 +462,7 @@
         block = (HALVES, batch, half)
         scratch = [
             pltpu.VMEM((2, places, GATES, HALVES, chunk, half), BF16),
+            pltpu.VMEM((2, places, HALVES, chunk, 2, half), BF16),
             pltpu.VMEM((2 * CORES, steps, *block), BF16),
             pltpu.VMEM((2, chips, 3, *block), F32),
             pltpu.VMEM((steps, chips, 3, *block), F32),
@@ -439,14 +476,14 @@
             pltpu.VMEM((2, 3, *block), F32),
             pltpu.VMEM((HALVES, steps, batch, half), BF16),
             pltpu.VMEM((HALVES, 2, batch, half), F32),
-            dma((2, places)),
-            dma((chips, 2)),
+            dma((2, 3, places)),
+            dma((3, chips, 2)),
             dma((2 * CORES,)),
             dma((chips, 2 * CORES)),
             dma((steps, chips)),
             dma((HALVES,)),
-            dma((2, chips, 2)),
-            dma((chips, 2)),
+            dma((2, 3, chips, 2)),
+            dma((3, chips, 2)),
             dma((2,)),
             dma((chips, 2)),
             dma((2, chips)),
@@ -471,8 +508,8 @@
             ),
         )(
             x_rows, h_rows,
-            jnp.transpose(wx_l1, (1, 0, 2)), jnp.transpose(whru_l1, (1, 0, 2)), whn_l1, bias_l1,
-            jnp.transpose(wx_l2, (1, 0, 2)), jnp.transpose(whru_l2, (1, 0, 2)), whn_l2, bias_l2,
+            jnp.transpose(wx_l1, (1, 0, 2)), whru_l1, whn_l1, bias_l1,
+            jnp.transpose(wx_l2, (1, 0, 2)), whru_l2, whn_l2, bias_l2,
         )
 
     seq_spec = P(None, "data", "row")

time: 396 us -> 389 us (0.982)
  local copies, waits for them, and re-layouts: 8.46 us -> 2.99 us
    transpose x1 -> x0, local copies, waits for them, and re-layouts: 5.47 us -> none  [device_body(): jnp.transpose(whru_l2, (1, 0, 2))]
where the time goes in v8:
time: 389 us
  Pallas kernels  385 us (99%)
    pallas_call x1, Pallas kernels, device_body(): pl.pallas_call(functools.partial(gru_kernel, rows, cols), name='gru', out...  385 us

profile of v8, /device:TPU:97, one launch (start us, length us, event | category | flops | bytes accessed | tf_op | source)
XLA Modules:
  0.0 388.8 jit_solution(13678438578077096801)
XLA Ops:
  0.6 385.1 %gru.1 = (bf16[24,32,128]{2,1,0:T(8,128)(2,1)}, f32[2,32,128]{2,1,0:T(8,128)}) custom-call(bf16[24,32,512]{2,1,0:T(8,128)(2,1)} %x_ref.1, f32[2,32,512]{2,1,0:T(8,128)} %h_ref.1, bf16[3,512,1024]{2,1,0:T(8,128)(2,1)} %bitcast.2, bf16[512,2,1024]{2,1,0:T(2,128)(2,1)} %wru1.1, bf16[512,1024]{1,0:T(8,128)(2,1)} %wn1.1, f32[3,1024]{1,0:T(4,128)} %b1.1, ...), custom_call_target="tpu_custom_call" | custom-call | tf_op jit(solution)/shard_map/gru/pallas_call | solution.py:496
  385.8 1.6 copy.14
  387.4 1.4 copy.15

commit v9 on v8

--- a/solution.py
+++ b/solution.py
@@ -31,7 +31,7 @@
     states, updates, projections, seq_halves, last_halves,
     weight_sem, hand_sem, x_sem, wide_sem, parts_sem, state_sem,
     weight_sent, handed_sent, x_sent, wide_sent, made_sent, state_sent,
-    block_sem, block_sent, out_sem, out_sent,
+    block_sem, block_sent, out_sem, out_sent, go_sem,
 ):
     chips = rows // CORES
     steps, batch, half = seq_out.shape
@@ -166,9 +166,9 @@
     def wide(parts):
         return jnp.concatenate(parts, axis=1)
 
-    def make_first(t, again):
+    def make_first(t, again, turns=None):
         slot = lax.rem(t, 2)
-        for turn in (2, 1, chips - 1, 0):
+        for turn in turns or (2, 1, chips - 1, 0):
             made = first_made.at[slot, turn]
             if again:
                 pltpu.make_async_copy(made, made, made_sent.at[slot, turn]).wait()
@@ -397,14 +397,22 @@
         split_pairs(1)
         weights_arrived(WX, 1)
 
+        def let_go(t):
+            def signal():
+                pl.semaphore_signal(go_sem, inc=1, device_id=device(xpos, 0, col), device_id_type=MESH)
+
+            pl.when(t + EARLY < steps)(signal)
+
         def step(t, first):
             first_reset(t)
             second_inputs(t)
             second_reset(t - 1)
+            let_go(t)
             first_next(t)
             if first:
                 weights_arrived(WN, 1)
             second_next(t - 1, False)
+            let_go(t)
             pl.when(t + 1 < steps)(lambda: first_inputs(t + 1))
 
         def later_step(t, carry):
@@ -434,11 +442,15 @@
 
     @pl.when(core == 0)
     def _():
+        make_first(EARLY, True)
+
         def later_first(t, carry):
-            make_first(t, True)
+            for turns in ((2,), (1, chips - 1, 0)):
+                pl.semaphore_wait(go_sem, 1)
+                make_first(t, True, turns)
             return carry
 
-        lax.fori_loop(EARLY, steps, later_first, 0)
+        lax.fori_loop(EARLY + 1, steps, later_first, 0)
         pltpu.make_async_copy(seq_out, seq_out, out_sem.at[0]).wait()
         pltpu.make_async_copy(last_out, last_out, out_sem.at[1]).wait()
 
@@ -492,6 +504,7 @@
             dma((kinds,)),
             dma((2,)),
             dma((2,)),
+            pltpu.SemaphoreType.REGULAR,
         ]
         return pl.pallas_call(
             functools.partial(gru_kernel, rows, cols),

time: 389 us -> 393 us (1.010)
  Pallas kernels: 385 us -> 389 us
    pallas_call x1, Pallas kernels: 385 us -> 389 us  [device_body(): pl.pallas_call(functools.partial(gru_kernel, rows, cols), name='gru', out...]
where the time goes in v9:
time: 393 us
  Pallas kernels  389 us (99%)
    pallas_call x1, Pallas kernels, device_body(): pl.pallas_call(functools.partial(gru_kernel, rows, cols), name='gru', out...  389 us

profile of v9, /device:TPU:97, one launch (start us, length us, event | category | flops | bytes accessed | tf_op | source)
XLA Modules:
  0.0 392.7 jit_solution(7059821039808100810)
XLA Ops:
  0.6 389.1 %gru.1 = (bf16[24,32,128]{2,1,0:T(8,128)(2,1)}, f32[2,32,128]{2,1,0:T(8,128)}) custom-call(bf16[24,32,512]{2,1,0:T(8,128)(2,1)} %x_ref.1, f32[2,32,512]{2,1,0:T(8,128)} %h_ref.1, bf16[3,512,1024]{2,1,0:T(8,128)(2,1)} %bitcast.2, bf16[512,2,1024]{2,1,0:T(2,128)(2,1)} %wru1.1, bf16[512,1024]{1,0:T(8,128)(2,1)} %wn1.1, f32[3,1024]{1,0:T(4,128)} %b1.1, ...), custom_call_target="tpu_custom_call" | custom-call | tf_op jit(solution)/shard_map/gru/pallas_call | solution.py:509
  389.7 1.6 copy.14
  391.3 1.4 copy.15

commit v10 on v8

--- a/solution.py
+++ b/solution.py
@@ -24,14 +24,14 @@
 
 def gru_kernel(
     rows, cols,
-    x_ref, h_ref, wx1, wru1, wn1, b1, wx2, wru2, wn2, b2,
+    x_ref, h_ref, wx1, wru1, wn1, b1_ref, wx2, wru2, wn2, b2_ref,
     seq_out, last_out,
     weights, pairs, x_here, first_made, first_parts, state_in,
     h1_blocks, r1_blocks, h2_blocks, r2_blocks,
-    states, updates, projections, seq_halves, last_halves,
+    states, updates, projections, seq_halves, last_halves, b1, b2,
     weight_sem, hand_sem, x_sem, wide_sem, parts_sem, state_sem,
     weight_sent, handed_sent, x_sent, wide_sent, made_sent, state_sent,
-    block_sem, block_sent, out_sem, out_sent,
+    block_sem, block_sent, out_sem, out_sent, bias_sem,
 ):
     chips = rows // CORES
     steps, batch, half = seq_out.shape
@@ -52,6 +52,9 @@
 
     def place_of(x_from, y_from, x_to, y_to):
         return chips * wrap_y(y_from - y_to) + wrap_x(x_from - x_to)
+
+    for n, (src, dst) in enumerate(((b1_ref, b1), (b2_ref, b2))):
+        pltpu.make_async_copy(src, dst, bias_sem.at[n]).start()
 
     barrier = pltpu.get_barrier_semaphore()
     for k in range(1, rows * cols):
@@ -230,6 +233,9 @@
             send_part(part, 1, (0,))
             send_handed(part)
 
+    for n, dst in enumerate((b1, b2)):
+        pltpu.make_async_copy(dst, dst, bias_sem.at[n]).wait()
+
     def drain_sends():
         for layer in range(2):
             for part in moving[layer]:
@@ -419,16 +425,22 @@
         all_sent(last_slot, H1)
         second_inputs(steps)
         second_reset(steps - 1)
-        second_next(steps - 1, True)
+        before, at_end = pl.ds(0, steps - 1), steps - 1
+        beside = device(xpos, 0, col)
+        early_copy = remote(seq_halves.at[0, before], seq_out.at[before], out_sent.at[2], out_sem.at[2], beside)
+        early_copy.start()
+        seq_out[before] = seq_halves[1, before]
+        second_next(at_end, True)
         for layer in range(2):
             for s in range(HALVES):
                 last_halves[s, layer] = states[layer, s]
-        seq_copy = remote(seq_halves.at[0], seq_out, out_sent.at[0], out_sem.at[0], device(xpos, 0, col))
-        last_copy = remote(last_halves.at[0], last_out, out_sent.at[1], out_sem.at[1], device(xpos, 0, col))
+        seq_copy = remote(seq_halves.at[0, at_end], seq_out.at[at_end], out_sent.at[0], out_sem.at[0], beside)
+        last_copy = remote(last_halves.at[0], last_out, out_sent.at[1], out_sem.at[1], beside)
         seq_copy.start()
         last_copy.start()
-        seq_out[...] = seq_halves[1]
+        seq_out[at_end] = seq_halves[1, at_end]
         last_out[...] = last_halves[1]
+        early_copy.wait_send()
         seq_copy.wait_send()
         last_copy.wait_send()
 
@@ -439,10 +451,16 @@
             return carry
 
         lax.fori_loop(EARLY, steps, later_first, 0)
-        pltpu.make_async_copy(seq_out, seq_out, out_sem.at[0]).wait()
+        for part, n in ((seq_out.at[pl.ds(0, steps - 1)], 2), (seq_out.at[steps - 1], 0)):
+            pltpu.make_async_copy(part, part, out_sem.at[n]).wait()
         pltpu.make_async_copy(last_out, last_out, out_sem.at[1]).wait()
 
     drain_sends()
+
+
+def pass_on(seq_ref, last_ref, seq_out, last_out):
+    seq_out[...] = seq_ref[...]
+    last_out[...] = last_ref[...]
 
 
 def solution(mesh):
@@ -476,6 +494,8 @@
             pltpu.VMEM((2, 3, *block), F32),
             pltpu.VMEM((HALVES, steps, batch, half), BF16),
             pltpu.VMEM((HALVES, 2, batch, half), F32),
+            pltpu.VMEM((3, col_block), F32),
+            pltpu.VMEM((3, col_block), F32),
             dma((2, 3, places)),
             dma((3, chips, 2)),
             dma((2 * CORES,)),
@@ -490,17 +510,19 @@
             dma((2, HALVES)),
             dma((kinds, places)),
             dma((kinds,)),
-            dma((2,)),
+            dma((3,)),
+            dma((3,)),
             dma((2,)),
         ]
-        return pl.pallas_call(
+        out_shape = (
+            jax.ShapeDtypeStruct((steps, batch, half), BF16),
+            jax.ShapeDtypeStruct((2, batch, half), F32),
+        )
+        results = pl.pallas_call(
             functools.partial(gru_kernel, rows, cols),
             name="gru",
-            out_shape=(
-                jax.ShapeDtypeStruct((steps, batch, half), BF16),
-                jax.ShapeDtypeStruct((2, batch, half), F32),
-            ),
-            in_specs=[anywhere, anywhere, anywhere, anywhere, anywhere, vmem, anywhere, anywhere, anywhere, vmem],
+            out_shape=out_shape,
+            in_specs=[anywhere] * 10,
             out_specs=(vmem, vmem),
             scratch_shapes=scratch,
             compiler_params=pltpu.CompilerParams(
@@ -511,6 +533,7 @@
             jnp.transpose(wx_l1, (1, 0, 2)), whru_l1, whn_l1, bias_l1,
             jnp.transpose(wx_l2, (1, 0, 2)), whru_l2, whn_l2, bias_l2,
         )
+        return pl.pallas_call(pass_on, name="results", out_shape=out_shape, in_specs=[vmem] * 2, out_specs=(vmem, vmem))(*results)
 
     seq_spec = P(None, "data", "row")
     out_spec = P(None, "data", ("col", "row"))

time: 389 us -> 386 us (level)
  no operation moved by 1% of the time
where the time goes in v10:
time: 386 us
  Pallas kernels  385 us (100%)
    pallas_call x1, Pallas kernels, device_body(): pl.pallas_call(functools.partial(gru_kernel, rows, cols), name='gru', out...  384 us

profile of v10, /device:TPU:97, one launch (start us, length us, event | category | flops | bytes accessed | tf_op | source)
XLA Modules:
  0.0 386.0 jit_solution(17209601537190019089)
XLA Ops:
  0.6 383.8 %gru.1 = (bf16[24,32,128]{2,1,0:T(8,128)(2,1)}, f32[2,32,128]{2,1,0:T(8,128)}) custom-call(bf16[24,32,512]{2,1,0:T(8,128)(2,1)} %x_ref.1, f32[2,32,512]{2,1,0:T(8,128)} %h_ref.1, bf16[3,512,1024]{2,1,0:T(8,128)(2,1)} %bitcast.2, bf16[512,2,1024]{2,1,0:T(2,128)(2,1)} %wru1.1, bf16[512,1024]{1,0:T(8,128)(2,1)} %wn1.1, f32[3,1024]{1,0:T(4,128)} %b1_ref.1, ...), custom_call_target="tpu_custom_call" | custom-call | tf_op jit(solution)/shard_map/gru/pallas_call | solution.py:521
  384.4 1.6 results.1

commit v11 on v10

--- a/solution.py
+++ b/solution.py
@@ -273,7 +273,7 @@
     distance = [ring_distance(dx, chips) + ring_distance(dy, cols) for dx, dy in offsets]
     far_first = sorted(range(1, places), key=lambda p: -distance[p])
     by_arrival = sorted(range(places), key=lambda p: (distance[p], ring_distance(offsets[p][0], chips)))
-    groups = [by_arrival[:6], by_arrival[6:10], by_arrival[10:]]
+    groups = [by_arrival[:6], by_arrival[6:10], by_arrival[10:14], by_arrival[14:]]
 
     def spread(blocks, kind):
         for p in far_first:
@@ -400,11 +400,11 @@
         first_reset(0)
         first_next(0)
         first_inputs(1)
-        split_pairs(1)
-        weights_arrived(WX, 1)
-
         def step(t, first):
             first_reset(t)
+            if first:
+                split_pairs(1)
+                weights_arrived(WX, 1)
             second_inputs(t)
             second_reset(t - 1)
             first_next(t)

time: 386 us -> 387 us (level)
  no operation moved by 1% of the time
where the time goes in v11:
time: 387 us
  Pallas kernels  386 us (100%)
    pallas_call x1, Pallas kernels, device_body(): pl.pallas_call(functools.partial(gru_kernel, rows, cols), name='gru', out...  385 us

profile of v11, /device:TPU:97, one launch (start us, length us, event | category | flops | bytes accessed | tf_op | source)
XLA Modules:
  0.0 386.8 jit_solution(15194659370417854160)
XLA Ops:
  0.6 384.5 %gru.1 = (bf16[24,32,128]{2,1,0:T(8,128)(2,1)}, f32[2,32,128]{2,1,0:T(8,128)}) custom-call(bf16[24,32,512]{2,1,0:T(8,128)(2,1)} %x_ref.1, f32[2,32,512]{2,1,0:T(8,128)} %h_ref.1, bf16[3,512,1024]{2,1,0:T(8,128)(2,1)} %bitcast.2, bf16[512,2,1024]{2,1,0:T(2,128)(2,1)} %wru1.1, bf16[512,1024]{1,0:T(8,128)(2,1)} %wn1.1, f32[3,1024]{1,0:T(4,128)} %b1_ref.1, ...), custom_call_target="tpu_custom_call" | custom-call | tf_op jit(solution)/shard_map/gru/pallas_call | solution.py:521
  385.2 1.6 results.1

commit v12 on v10

--- a/solution.py
+++ b/solution.py
@@ -26,10 +26,10 @@
     rows, cols,
     x_ref, h_ref, wx1, wru1, wn1, b1_ref, wx2, wru2, wn2, b2_ref,
     seq_out, last_out,
-    weights, pairs, x_here, first_made, first_parts, state_in,
+    weights, pairs, x_here, first_made, first_passed, first_parts, state_in,
     h1_blocks, r1_blocks, h2_blocks, r2_blocks,
     states, updates, projections, seq_halves, last_halves, b1, b2,
-    weight_sem, hand_sem, x_sem, wide_sem, parts_sem, state_sem,
+    weight_sem, hand_sem, x_sem, wide_sem, passed_sem, parts_sem, state_sem,
     weight_sent, handed_sent, x_sent, wide_sent, made_sent, state_sent,
     block_sem, block_sent, out_sem, out_sent, bias_sem,
 ):
@@ -169,25 +169,39 @@
     def wide(parts):
         return jnp.concatenate(parts, axis=1)
 
-    def make_first(t, again):
-        slot = lax.rem(t, 2)
-        for turn in (2, 1, chips - 1, 0):
-            made = first_made.at[slot, turn]
-            if again:
-                pltpu.make_async_copy(made, made, made_sent.at[slot, turn]).wait()
+    def make_first(t, way, again):
+        onward, other = ((1, chips - 1), (chips - 1, 1))[way]
+
+        def part_of(turn):
             total = None
             for n in range(2 * CORES):
                 rhs = wide([weights[0, 2 * CORES * turn + n, g, s] for g in range(3) for s in range(HALVES)])
                 lhs = wide([x_here[n, t, s] for s in range(HALVES)])
                 term = jnp.dot(lhs, rhs, preferred_element_type=F32)
                 total = term if total is None else total + term
+            return total
+
+        def emit(turn, passed, dst, sem, to):
+            made = first_made.at[way, turn]
+            if again:
+                pltpu.make_async_copy(made, made, made_sent.at[way, turn]).wait()
+            total = part_of(turn)
+            if passed is not None:
+                pltpu.make_async_copy(passed, passed, passed_sem.at[way]).wait()
             for g in range(3):
                 for s in range(HALVES):
                     n = g * HALVES + s
-                    made[g, s] = total[:, n * half : (n + 1) * half]
-            seen = (chips - turn) % chips
-            to = device(wrap_x(xpos + turn), 1, col)
-            remote(made, first_parts.at[t, seen], made_sent.at[slot, turn], parts_sem.at[t, seen], to).start()
+                    value = total[:, n * half : (n + 1) * half]
+                    made[g, s] = value if passed is None else value + passed[g, s]
+            remote(made, dst, made_sent.at[way, turn], sem, to).start()
+
+        def parts(seen):
+            return first_parts.at[t, seen], parts_sem.at[t, seen]
+
+        emit(2, None, first_passed.at[way], passed_sem.at[way], device(wrap_x(xpos + onward), 0, col))
+        emit(other, None, *parts(1 - way), device(wrap_x(xpos + other), 1, col))
+        emit(onward, first_passed.at[way], *parts(way), device(wrap_x(xpos + onward), 1, col))
+        emit(0, None, *parts(2), device(xpos, 1, col))
 
     far_turns = (2, 1, chips - 1)
 
@@ -227,7 +241,7 @@
             send_part(part, 0, (0,))
         inputs_here()
         for t in range(EARLY):
-            make_first(t, False)
+            make_first(t, t % 2, False)
         for part in moving[1]:
             send_part(part, 1, far_turns)
             send_part(part, 1, (0,))
@@ -351,13 +365,13 @@
         all_sent(r1_blocks, R1)
 
     def first_inputs(t):
-        for n in range(chips):
+        for n in range(3):
             part = first_parts.at[t, n]
             pltpu.make_async_copy(part, part, parts_sem.at[t, n]).wait()
         for g in range(3):
             for s in range(HALVES):
                 here = b1[pl.ds(g, 1), pl.ds(pl.multiple_of(xpos * chunk + s * half, half), half)]
-                projections[0, g, s] = sum(first_parts[t, n, g, s] for n in range(chips)) + here
+                projections[0, g, s] = sum(first_parts[t, n, g, s] for n in range(3)) + here
 
     def second_inputs(t):
         slot = h1_blocks.at[lax.rem(t, 2)]
@@ -446,11 +460,12 @@
 
     @pl.when(core == 0)
     def _():
-        def later_first(t, carry):
-            make_first(t, True)
+        def later_first(pair, carry):
+            for way in range(2):
+                make_first(2 * pair + way, way, True)
             return carry
 
-        lax.fori_loop(EARLY, steps, later_first, 0)
+        lax.fori_loop(EARLY // 2, steps // 2, later_first, 0)
         for part, n in ((seq_out.at[pl.ds(0, steps - 1)], 2), (seq_out.at[steps - 1], 0)):
             pltpu.make_async_copy(part, part, out_sem.at[n]).wait()
         pltpu.make_async_copy(last_out, last_out, out_sem.at[1]).wait()
@@ -483,7 +498,8 @@
             pltpu.VMEM((2, places, HALVES, chunk, 2, half), BF16),
             pltpu.VMEM((2 * CORES, steps, *block), BF16),
             pltpu.VMEM((2, chips, 3, *block), F32),
-            pltpu.VMEM((steps, chips, 3, *block), F32),
+            pltpu.VMEM((2, 3, *block), F32),
+            pltpu.VMEM((steps, 3, 3, *block), F32),
             pltpu.VMEM((2, *block), F32),
             pltpu.VMEM((2, places, *block), BF16),
             pltpu.VMEM((places, *block), BF16),
@@ -500,7 +516,8 @@
             dma((3, chips, 2)),
             dma((2 * CORES,)),
             dma((chips, 2 * CORES)),
-            dma((steps, chips)),
+            dma((2,)),
+            dma((steps, 3)),
             dma((HALVES,)),
             dma((2, 3, chips, 2)),
             dma((3, chips, 2)),

time: 386 us -> 380 us (0.984)
  Pallas kernels: 385 us -> 380 us
    pallas_call x1, Pallas kernels: 384 us -> 378 us  [device_body(): pl.pallas_call(functools.partial(gru_kernel, rows, cols), name='gru', out...]
where the time goes in v12:
time: 380 us
  Pallas kernels  380 us (100%)
    pallas_call x1, Pallas kernels, device_body(): pl.pallas_call(functools.partial(gru_kernel, rows, cols), name='gru', out...  378 us

profile of v12, /device:TPU:97, one launch (start us, length us, event | category | flops | bytes accessed | tf_op | source)
XLA Modules:
  0.0 380.3 jit_solution(13428802646574633301)
XLA Ops:
  0.6 378.0 %gru.1 = (bf16[24,32,128]{2,1,0:T(8,128)(2,1)}, f32[2,32,128]{2,1,0:T(8,128)}) custom-call(bf16[24,32,512]{2,1,0:T(8,128)(2,1)} %x_ref.1, f32[2,32,512]{2,1,0:T(8,128)} %h_ref.1, bf16[3,512,1024]{2,1,0:T(8,128)(2,1)} %bitcast.2, bf16[512,2,1024]{2,1,0:T(2,128)(2,1)} %wru1.1, bf16[512,1024]{1,0:T(8,128)(2,1)} %wn1.1, f32[3,1024]{1,0:T(4,128)} %b1_ref.1, ...), custom_call_target="tpu_custom_call" | custom-call | tf_op jit(solution)/shard_map/gru/pallas_call | solution.py:538
  378.7 1.6 results.1

commit v13 on v12

--- a/solution.py
+++ b/solution.py
@@ -285,7 +285,11 @@
 
     offsets = [(dx, dy) for dy in range(cols) for dx in range(chips)]
     distance = [ring_distance(dx, chips) + ring_distance(dy, cols) for dx, dy in offsets]
-    far_first = sorted(range(1, places), key=lambda p: -distance[p])
+    def weight_of(p):
+        in_x, in_y = ring_distance(offsets[p][0], chips), ring_distance(offsets[p][1], cols)
+        return -distance[p], -in_y if distance[p] > 1 else -in_x
+
+    far_first = sorted(range(1, places), key=weight_of)
     by_arrival = sorted(range(places), key=lambda p: (distance[p], ring_distance(offsets[p][0], chips)))
     groups = [by_arrival[:6], by_arrival[6:10], by_arrival[10:]]
 

time: 380 us -> 380 us (level)
  no operation moved by 1% of the time
where the time goes in v13:
time: 380 us
  Pallas kernels  380 us (100%)
    pallas_call x1, Pallas kernels, device_body(): pl.pallas_call(functools.partial(gru_kernel, rows, cols), name='gru', out...  378 us

profile of v13, /device:TPU:97, one launch (start us, length us, event | category | flops | bytes accessed | tf_op | source)
XLA Modules:
  0.0 380.3 jit_solution(10404442048590248960)
XLA Ops:
  0.6 378.1 %gru.1 = (bf16[24,32,128]{2,1,0:T(8,128)(2,1)}, f32[2,32,128]{2,1,0:T(8,128)}) custom-call(bf16[24,32,512]{2,1,0:T(8,128)(2,1)} %x_ref.1, f32[2,32,512]{2,1,0:T(8,128)} %h_ref.1, bf16[3,512,1024]{2,1,0:T(8,128)(2,1)} %bitcast.2, bf16[512,2,1024]{2,1,0:T(2,128)(2,1)} %wru1.1, bf16[512,1024]{1,0:T(8,128)(2,1)} %wn1.1, f32[3,1024]{1,0:T(4,128)} %b1_ref.1, ...), custom_call_target="tpu_custom_call" | custom-call | tf_op jit(solution)/shard_map/gru/pallas_call | solution.py:542
  378.7 1.6 results.1

commit v14 on v12

--- a/solution.py
+++ b/solution.py
@@ -320,23 +320,25 @@
             total = product(lambda p, s: blocks[p, s], layer, (gate,), group, total)
         return total
 
-    def project(layer, lhs_of, bias):
-        total = product(lhs_of, layer, (RESET, UPDATE, CAND), range(places))
-        for g in range(3):
-            for s in range(HALVES):
-                n = g * HALVES + s
+    def project(layer, lhs_of, bias, gates):
+        total = product(lhs_of, layer, gates, range(places))
+        for k, g in enumerate(gates):
+            for s in range(HALVES):
+                n = k * HALVES + s
                 here = bias[pl.ds(g, 1), pl.ds(pl.multiple_of(xpos * chunk + s * half, half), half)]
                 projections[layer, g, s] = total[:, n * half : (n + 1) * half] + here
 
-    def reset_half(layer, blocks, kind, out_blocks, send):
+    def reset_half(layer, blocks, kind, out_blocks):
         total = gathered(blocks, kind, layer, REC_RESET)
         for s in range(HALVES):
             reset = jax.nn.sigmoid(projections[layer, RESET, s] + total[:, s * half : (s + 1) * half])
             out_blocks[0, s] = (reset * states[layer, s]).astype(BF16)
-        send()
+
+    def update_half(layer, blocks, kind):
         total = product(lambda p, s: blocks[p, s], layer, (REC_UPDATE,), range(places))
         for s in range(HALVES):
             updates[layer, s] = jax.nn.sigmoid(projections[layer, UPDATE, s] + total[:, s * half : (s + 1) * half])
+        all_sent(blocks, kind)
 
     def next_half(layer, blocks, kind, emit):
         total = gathered(blocks, kind, layer, REC_CAND)
@@ -350,9 +352,11 @@
     H1, R1, H2, R2 = range(4)
 
     def first_reset(t):
-        slot = h1_blocks.at[lax.rem(t, 2)]
-        reset_half(0, slot, H1, r1_blocks, lambda: spread(r1_blocks, R1))
-        all_sent(slot, H1)
+        reset_half(0, h1_blocks.at[lax.rem(t, 2)], H1, r1_blocks)
+        spread(r1_blocks, R1)
+
+    def first_update(t):
+        update_half(0, h1_blocks.at[lax.rem(t, 2)], H1)
 
     def first_next(t):
         slot = h1_blocks.at[lax.rem(t + 1, 2)]
@@ -373,14 +377,16 @@
                 here = b1[pl.ds(g, 1), pl.ds(pl.multiple_of(xpos * chunk + s * half, half), half)]
                 projections[0, g, s] = sum(first_parts[t, n, g, s] for n in range(3)) + here
 
-    def second_inputs(t):
+    def second_inputs(t, gates):
         slot = h1_blocks.at[lax.rem(t, 2)]
-        project(1, lambda p, s: slot[p, s], b2)
+        project(1, lambda p, s: slot[p, s], b2, gates)
 
     def second_reset(t):
-        slot = h2_blocks.at[lax.rem(t, 2)]
-        reset_half(1, slot, H2, r2_blocks, lambda: spread(r2_blocks, R2))
-        all_sent(slot, H2)
+        reset_half(1, h2_blocks.at[lax.rem(t, 2)], H2, r2_blocks)
+        spread(r2_blocks, R2)
+
+    def second_update(t):
+        update_half(1, h2_blocks.at[lax.rem(t, 2)], H2)
 
     def second_next(t, last):
         slot = h2_blocks.at[lax.rem(t + 1, 2)]
@@ -412,6 +418,7 @@
         weights_arrived(WN, 0)
         first_inputs(0)
         first_reset(0)
+        first_update(0)
         first_next(0)
         first_inputs(1)
         split_pairs(1)
@@ -419,8 +426,11 @@
 
         def step(t, first):
             first_reset(t)
-            second_inputs(t)
+            second_inputs(t, (RESET,))
             second_reset(t - 1)
+            first_update(t)
+            second_inputs(t, (UPDATE, CAND))
+            second_update(t - 1)
             first_next(t)
             if first:
                 weights_arrived(WN, 1)
@@ -437,8 +447,10 @@
         for p in range(1, places):
             arrived(last_slot, H1, p)
         all_sent(last_slot, H1)
-        second_inputs(steps)
+        second_inputs(steps, (RESET,))
         second_reset(steps - 1)
+        second_inputs(steps, (UPDATE, CAND))
+        second_update(steps - 1)
         before, at_end = pl.ds(0, steps - 1), steps - 1
         beside = device(xpos, 0, col)
         early_copy = remote(seq_halves.at[0, before], seq_out.at[before], out_sent.at[2], out_sem.at[2], beside)

time: 380 us -> 384 us (1.011)
  Pallas kernels: 380 us -> 384 us
    pallas_call x1, Pallas kernels: 378 us -> 382 us  [device_body(): pl.pallas_call(functools.partial(gru_kernel, rows, cols), name='gru', out...]
where the time goes in v14:
time: 384 us
  Pallas kernels  384 us (100%)
    pallas_call x1, Pallas kernels, device_body(): pl.pallas_call(functools.partial(gru_kernel, rows, cols), name='gru', out...  382 us

profile of v14, /device:TPU:97, one launch (start us, length us, event | category | flops | bytes accessed | tf_op | source)
XLA Modules:
  0.0 384.4 jit_solution(2230717516500680182)
XLA Ops:
  0.6 382.1 %gru.1 = (bf16[24,32,128]{2,1,0:T(8,128)(2,1)}, f32[2,32,128]{2,1,0:T(8,128)}) custom-call(bf16[24,32,512]{2,1,0:T(8,128)(2,1)} %x_ref.1, f32[2,32,512]{2,1,0:T(8,128)} %h_ref.1, bf16[3,512,1024]{2,1,0:T(8,128)(2,1)} %bitcast.2, bf16[512,2,1024]{2,1,0:T(2,128)(2,1)} %wru1.1, bf16[512,1024]{1,0:T(8,128)(2,1)} %wn1.1, f32[3,1024]{1,0:T(4,128)} %b1_ref.1, ...), custom_call_target="tpu_custom_call" | custom-call | tf_op jit(solution)/shard_map/gru/pallas_call | solution.py:550
  382.8 1.6 results.1

commit v15 on v12

--- a/solution.py
+++ b/solution.py
@@ -414,29 +414,31 @@
         first_reset(0)
         first_next(0)
         first_inputs(1)
+        first_reset(1)
+        first_next(1)
         split_pairs(1)
         weights_arrived(WX, 1)
-
-        def step(t, first):
+        second_inputs(1)
+        second_reset(0)
+
+        first_inputs(2)
+
+        def step(t, carry):
             first_reset(t)
+            pl.when(t == 2)(lambda: weights_arrived(WN, 1))
+            second_next(t - 2, False)
+            first_next(t)
             second_inputs(t)
             second_reset(t - 1)
-            first_next(t)
-            if first:
-                weights_arrived(WN, 1)
-            second_next(t - 1, False)
             pl.when(t + 1 < steps)(lambda: first_inputs(t + 1))
-
-        def later_step(t, carry):
-            step(t, False)
             return carry
 
-        step(1, True)
-        lax.fori_loop(2, steps, later_step, 0)
+        lax.fori_loop(2, steps, step, 0)
         last_slot = h1_blocks.at[steps % 2]
         for p in range(1, places):
             arrived(last_slot, H1, p)
         all_sent(last_slot, H1)
+        second_next(steps - 2, False)
         second_inputs(steps)
         second_reset(steps - 1)
         before, at_end = pl.ds(0, steps - 1), steps - 1

time: 380 us -> 385 us (1.013)
  Pallas kernels: 380 us -> 384 us
    pallas_call x1, Pallas kernels: 378 us -> 382 us  [device_body(): pl.pallas_call(functools.partial(gru_kernel, rows, cols), name='gru', out...]
where the time goes in v15:
time: 385 us
  Pallas kernels  384 us (100%)
    pallas_call x1, Pallas kernels, device_body(): pl.pallas_call(functools.partial(gru_kernel, rows, cols), name='gru', out...  382 us

profile of v15, /device:TPU:97, one launch (start us, length us, event | category | flops | bytes accessed | tf_op | source)
XLA Modules:
  0.0 384.7 jit_solution(624600243575449957)
XLA Ops:
  0.6 382.4 %gru.1 = (bf16[24,32,128]{2,1,0:T(8,128)(2,1)}, f32[2,32,128]{2,1,0:T(8,128)}) custom-call(bf16[24,32,512]{2,1,0:T(8,128)(2,1)} %x_ref.1, f32[2,32,512]{2,1,0:T(8,128)} %h_ref.1, bf16[3,512,1024]{2,1,0:T(8,128)(2,1)} %bitcast.2, bf16[512,2,1024]{2,1,0:T(2,128)(2,1)} %wru1.1, bf16[512,1024]{1,0:T(8,128)(2,1)} %wn1.1, f32[3,1024]{1,0:T(4,128)} %b1_ref.1, ...), custom_call_target="tpu_custom_call" | custom-call | tf_op jit(solution)/shard_map/gru/pallas_call | solution.py:540
  383.0 1.6 results.1
